TPU v7x, 32 devices: a whole 2x2x4 slice. The times are simulated.
32 devices in a mesh: grp: 2 (over y), kvp: 4 (over x, core), tp: 4 (over z).
Axes of the slice: x: 2, y: 2, z: 4, core: 2. Of those that a mesh axis runs over, the one named last changes fastest.
Arguments:
- hidden_in: bfloat16 [16, 7168], P('grp'), parts along dimension 0, may hold values from -3 to 3
- queries_nope: bfloat16 [16, 128, 128], P('grp', ('kvp', 'tp')), parts along dimension 0, may hold values from -6 to 6
- queries_rope: bfloat16 [16, 128, 64], P('grp', ('kvp', 'tp')), parts along dimension 0, may hold values from -26 to 26
- cache: bfloat16 [16, 1536, 576], P('grp', 'kvp'), parts along dimension 0, may hold values from -20 to 20
- lengths: int32 [16], P('grp'), parts along dimension 0, may hold values from 128 to 1536, as said below
- w_uk: bfloat16 [128, 128, 512], P(('kvp', 'tp')), may hold values from -0.5 to 0.5
- w_uv: bfloat16 [128, 512, 128], P(('kvp', 'tp')), may hold values from -0.25 to 0.25
- w_out: bfloat16 [16384, 7168], P(('kvp', 'tp')), may hold values from -0.0625 to 0.0625
- norm_gain: float32 [7168], replicated, may hold values from 0.25 to 1.75
- w_gate: bfloat16 [7168, 18432], P(None, ('kvp', 'tp')), may hold values from -0.0625 to 0.0625
- w_up: bfloat16 [7168, 18432], P(None, ('kvp', 'tp')), may hold values from -0.0625 to 0.0625
- w_down: bfloat16 [18432, 7168], P(('kvp', 'tp')), may hold values from -0.0625 to 0.0625
Outputs:
- layer_out: bfloat16 [16, 7168], P('grp', ('kvp', 'tp')), parts along dimension 0
There are 2 independent parts, one for each index of `grp`. A program takes and returns all parts, laid end to end along the dimension named above; an argument that names none is the same for every part. Nothing has to cross between parts.
Inputs may be any that keep to these rules, and one draw needn't show every extreme that they name: `lengths`: every length is a multiple of 128; in every draw some request has the full 1536.
All inputs are finite; a program needn't handle non-finite values.
Results may differ from a plain program's by a relative error of at most 0.04.
Values may be sent and summed in bfloat16 or wider, within the bound.
A program may use at most 128 MiB of HBM per device.

v0:
```python
import functools

import jax
import jax.numpy as jnp
from jax import lax
from jax.experimental import pallas as pl
from jax.experimental.pallas import tpu as pltpu
from jax.sharding import PartitionSpec as P


def project(o_lat, w_uv, w_out):
    head_out = jnp.einsum("bhl,hle->bhe", o_lat, w_uv, preferred_element_type=jnp.float32).astype(
        jnp.bfloat16
    )
    return jnp.dot(
        head_out.reshape(head_out.shape[0], -1), w_out, preferred_element_type=jnp.float32
    )


def plain_device(
    hidden_in,
    queries_nope,
    queries_rope,
    cache,
    lengths,
    w_uk,
    w_uv,
    w_out,
    norm_gain,
    w_gate,
    w_up,
    w_down,
):
    batch, heads_dev, head_dim = queries_nope.shape
    latent = w_uk.shape[2]
    ctx_dev = cache.shape[1]
    groups = lax.axis_size("kvp")
    score_scale = float(head_dim + queries_rope.shape[2]) ** (-0.5)
    q_lat = jnp.einsum(
        "bhd,hdl->bhl", queries_nope, w_uk, preferred_element_type=jnp.float32
    ).astype(jnp.bfloat16)
    q_lat_all, rope_all = (
        lax.all_gather(q_lat, "kvp", axis=1, tiled=True),
        lax.all_gather(queries_rope, "kvp", axis=1, tiled=True),
    )
    q_full = jnp.concatenate([q_lat_all, rope_all], axis=2)
    scores = (
        jnp.einsum("bhc,btc->bht", q_full, cache, preferred_element_type=jnp.float32) * score_scale
    )
    offset = lax.axis_index("kvp") * ctx_dev
    visible = ((offset + jnp.arange(ctx_dev, dtype=jnp.int32))[None, :] < lengths[:, None])[
        :, None, :
    ]
    masked = jnp.where(visible, scores, jnp.float32(-1e30))
    block_max = jnp.max(masked, axis=2)
    exponent = jnp.where(visible, jnp.exp(masked - block_max[..., None]), jnp.float32(0.0))
    guarded = jnp.maximum(jnp.sum(exponent, axis=2), 1.0)
    log_total = block_max + jnp.log(guarded)
    weights = (exponent / guarded[..., None]).astype(jnp.bfloat16)
    partial_value = jnp.einsum("bht,btc->bhc", weights, cache, preferred_element_type=jnp.float32)[
        ..., :latent
    ]
    blocks = partial_value.reshape(batch, groups, heads_dev, latent)
    block_logs = log_total.reshape(batch, groups, heads_dev)
    part_blocks = lax.all_to_all(
        blocks.astype(jnp.bfloat16), "kvp", split_axis=1, concat_axis=1, tiled=True
    ).astype(blocks.dtype)
    part_logs = lax.all_to_all(
        block_logs.astype(jnp.bfloat16), "kvp", split_axis=1, concat_axis=1, tiled=True
    ).astype(block_logs.dtype)
    highest = jnp.max(part_logs, axis=1)
    overall = highest + jnp.log(jnp.sum(jnp.exp(part_logs - highest[:, None, :]), axis=1))
    scaled = jnp.exp(part_logs - overall[:, None, :])[..., None] * part_blocks
    o_lat = jnp.sum(scaled, axis=1).astype(jnp.bfloat16)
    attention = project(o_lat, w_uv, w_out)
    model_width = norm_gain.shape[0]
    share_width = model_width // lax.axis_size(("kvp", "tp"))
    share_start = lax.axis_index(("kvp", "tp")) * share_width
    attn_whole = lax.psum(attention, ("kvp", "tp"))
    residual = hidden_in.astype(jnp.float32) + attn_whole
    mean_square = jnp.mean(residual * residual, axis=1)
    normed = (residual * lax.rsqrt(mean_square + 1e-06)[:, None] * norm_gain[None, :]).astype(
        jnp.bfloat16
    )
    residual_share = lax.dynamic_slice_in_dim(residual, share_start, share_width, 1)
    gate_proj = jnp.dot(normed, w_gate, preferred_element_type=jnp.float32)
    up_proj = jnp.dot(normed, w_up, preferred_element_type=jnp.float32)
    act = (jax.nn.silu(gate_proj) * up_proj).astype(jnp.bfloat16)
    ffn_terms = jnp.dot(act, w_down, preferred_element_type=jnp.float32)
    ffn_share = lax.psum_scatter(ffn_terms, ("kvp", "tp"), scatter_dimension=1, tiled=True)
    return (residual_share + ffn_share).astype(jnp.bfloat16)


MESH = pl.DeviceIdType.MESH
F32 = jnp.float32
BF16 = jnp.bfloat16
VMEM_BYTES = 67043328


def layer_kernel(
    groups, tps, share, chunk, out_rows,
    hidden_ref, nope_ref, rope_ref, len_ref, gain_ref,
    cache_hbm, uk_hbm, uv_hbm, wo_hbm, wg_hbm, wu_hbm, wd_hbm,
    out_ref,
    cache_v, uk_v, uv_v, big_v, wg_v, wu_v,
    nope_s, qlat_s, q_send, q_all, score_s, part_send, part_all, log_send, log_all,
    olat_s, head_s, hid_s, rs_send, rs_all, ag_send, ag_all, wide_s, norm_s, fs_send, fs_all,
    uk_sem, cache_sem, uv_sem, wo_sem, wg_sem, wu_sem, wd_sem,
    q_ss, q_rs, part_ss, part_rs, log_ss, log_rs, rs_ss, rs_rs, ag_ss, ag_rs, fs_ss, fs_rs,
):
    count = groups * tps
    kvp = lax.axis_index("kvp")
    tp = lax.axis_index("tp")
    me = kvp * tps + tp
    batch, heads, head_dim = nope_ref.shape
    latent = uk_v.shape[2]
    rope = rope_ref.shape[2]
    ctx = cache_v.shape[2]
    width = hidden_ref.shape[1]
    chunks = width // chunk
    per_chunk = chunk // share

    def peer(index):
        return {"kvp": index // tps, "tp": index % tps}

    def turn(step):
        return lax.rem(me // per_chunk + 1 + step, chunks)

    def load_uk():
        return pltpu.make_async_copy(uk_hbm, uk_v, uk_sem)

    def load_cache():
        return pltpu.make_async_copy(cache_hbm, cache_v, cache_sem)

    def load_uv():
        return pltpu.make_async_copy(uv_hbm, uv_v, uv_sem)

    def cols(j):
        return pl.ds(pl.multiple_of(j * chunk, 128), chunk)

    def load_wo(j):
        return pltpu.make_async_copy(
            wo_hbm.at[:, cols(j)], big_v.at[j, pl.ds(0, out_rows)], wo_sem.at[j]
        )

    def load_wd(j):
        return pltpu.make_async_copy(wd_hbm.at[:, cols(j)], big_v.at[j], wd_sem.at[j])

    def load_wg(j):
        return pltpu.make_async_copy(wg_hbm.at[cols(j)], wg_v.at[cols(j)], wg_sem.at[j])

    def load_wu(j):
        return pltpu.make_async_copy(wu_hbm.at[cols(j)], wu_v.at[cols(j)], wu_sem.at[j])

    load_uk().start()
    load_cache().start()

    barrier = pltpu.get_barrier_semaphore()

    @pl.loop(1, count)
    def _(d):
        pl.semaphore_signal(
            barrier, inc=1, device_id=peer(lax.rem(me + d, count)), device_id_type=MESH
        )

    nope_s[...] = nope_ref[...].astype(F32)
    for s in range(count):
        hid_s[s] = hidden_ref[:, s * share : (s + 1) * share].astype(F32)
    load_uk().wait()
    load_uv().start()

    @pl.loop(0, chunks)
    def _(step):
        load_wo(turn(step)).start()

    for i in range(heads):
        qlat_s[:, i, :] = jnp.dot(
            nope_s[:, i, :].astype(BF16), uk_v[i], preferred_element_type=F32
        )
    q_send[:, :, :latent] = qlat_s[...].astype(BF16)
    q_send[:, :, latent:] = rope_ref[...]
    pl.semaphore_wait(barrier, count - 1)

    def exchange(d, source, target, ss, rs, ahead):
        other = lax.rem(kvp + d, groups) if ahead else lax.rem(kvp + groups - d, groups)
        return pltpu.make_async_remote_copy(
            src_ref=source.at[other] if source is not q_send else source,
            dst_ref=target.at[kvp if ahead else other],
            send_sem=ss.at[d],
            recv_sem=rs.at[kvp if ahead else other],
            device_id={"kvp": other, "tp": tp},
            device_id_type=MESH,
        )

    for d in range(1, groups):
        exchange(d, q_send, q_all, q_ss, q_rs, True).start()

    @pl.loop(0, chunks)
    def _(j):
        load_wg(j).start()
        load_wu(j).start()

    q_all[kvp] = q_send[...]
    load_cache().wait()
    for d in range(1, groups):
        exchange(d, q_send, q_all, q_ss, q_rs, False).wait_recv()

    scale = float(head_dim + rope) ** (-0.5)
    rows = groups * heads
    for b in range(batch):
        q = q_all[:, b].astype(F32).reshape(rows, latent + rope)
        score_s[b] = (
            jnp.dot(
                q[:, :latent].astype(BF16), cache_v[b, :latent],
                preferred_element_type=F32,
            )
            + jnp.dot(
                q[:, latent:].astype(BF16), cache_v[b, latent:],
                preferred_element_type=F32,
            )
        ) * scale
    position = kvp * ctx + lax.broadcasted_iota(jnp.int32, (rows, ctx), 1)
    for b in range(batch):
        visible = position < len_ref[b]
        masked = jnp.where(visible, score_s[b], F32(-1e30))
        top = jnp.max(masked, axis=1, keepdims=True)
        exps = jnp.where(visible, jnp.exp(masked - top), F32(0.0))
        guarded = jnp.maximum(jnp.sum(exps, axis=1, keepdims=True), 1.0)
        log_total = jnp.broadcast_to(top + jnp.log(guarded), (rows, 128))
        weights = (exps / guarded).astype(BF16)
        part = lax.dot_general(
            weights, cache_v[b, :latent], (((1,), (1,)), ((), ())), preferred_element_type=F32
        )
        for g in range(groups):
            part_send[g, b] = part[g * heads : (g + 1) * heads].astype(BF16)
            log_send[g, b] = log_total[g * heads : (g + 1) * heads]

    for d in range(1, groups):
        exchange(d, log_send, log_all, log_ss, log_rs, True).start()
        exchange(d, part_send, part_all, part_ss, part_rs, True).start()
    part_all[kvp] = part_send[kvp]
    log_all[kvp] = log_send[kvp]
    load_uv().wait()
    for d in range(1, groups):
        exchange(d, log_send, log_all, log_ss, log_rs, False).wait_recv()
        exchange(d, part_send, part_all, part_ss, part_rs, False).wait_recv()

    logs = [log_all[g] for g in range(groups)]
    highest = functools.reduce(jnp.maximum, logs)
    overall = highest + jnp.log(sum(jnp.exp(x - highest) for x in logs))
    factors = [jnp.exp(x - overall) for x in logs]
    for c in range(0, latent, 128):
        olat_s[:, :, c : c + 128] = sum(
            factors[g] * part_all[g, :, :, c : c + 128].astype(F32) for g in range(groups)
        )
    for i in range(heads):
        head_s[:, i * head_dim : (i + 1) * head_dim] = jnp.dot(
            olat_s[:, i, :].astype(BF16), uv_v[i], preferred_element_type=F32
        ).astype(BF16)

    def scatter(d, source, target, ss, rs, ahead):
        other = lax.rem(me + d, count) if ahead else lax.rem(me + count - d, count)
        return pltpu.make_async_remote_copy(
            src_ref=source.at[other] if source is not ag_send else source,
            dst_ref=target.at[me if ahead else other],
            send_sem=ss.at[d],
            recv_sem=rs.at[me if ahead else other],
            device_id=peer(other),
            device_id_type=MESH,
        )

    def send_chunk(j, term, source, target, ss, rs):
        for p in range(per_chunk):
            owner = j * per_chunk + p
            source[owner] = term[:, p * share : (p + 1) * share].astype(BF16)
        for p in range(per_chunk):
            owner = j * per_chunk + p

            @pl.when(owner != me)
            def _():
                scatter(
                    lax.rem(owner - me + count, count), source, target, ss, rs, True
                ).start()

    def send_all(source, target, ss, rs):
        @pl.loop(1, count)
        def _(d):
            scatter(d, source, target, ss, rs, True).start()

    def receive_all(source, target, ss, rs):
        @pl.loop(1, count)
        def _(d):
            scatter(d, source, target, ss, rs, False).wait_recv()

    def sent_all(source, target, ss, rs):
        @pl.loop(1, count)
        def _(d):
            scatter(d, source, target, ss, rs, True).wait_send()

    @pl.loop(0, chunks)
    def _(step):
        j = turn(step)
        load_wo(j).wait()
        term = jnp.dot(head_s[...], big_v[j, :out_rows], preferred_element_type=F32)
        load_wd(j).start()
        send_chunk(j, term, rs_send, rs_all, rs_ss, rs_rs)

    rs_all[me] = rs_send[me]
    receive_all(rs_send, rs_all, rs_ss, rs_rs)
    residual = hid_s[me]
    for s in range(count):
        residual = residual + rs_all[s].astype(F32)
    hid_s[me] = residual
    ag_send[...] = residual.astype(BF16)
    send_all(ag_send, ag_all, ag_ss, ag_rs)
    ag_all[me] = ag_send[...]
    receive_all(ag_send, ag_all, ag_ss, ag_rs)

    square = jnp.zeros((batch, share), F32)
    for s in range(count):
        value = ag_all[s].astype(F32)
        square = square + value * value
        wide_s[:, s * share : (s + 1) * share] = value
    mean_square = jnp.sum(square, axis=1, keepdims=True) / width
    inverse = lax.rsqrt(mean_square + 1e-06)
    norm_s[...] = (wide_s[...] * inverse * gain_ref[...]).astype(BF16)

    def hidden_units(j, totals):
        load_wg(j).wait()
        load_wu(j).wait()
        x = norm_s[:, cols(j)]
        return (
            totals[0] + jnp.dot(x, wg_v[cols(j)], preferred_element_type=F32),
            totals[1] + jnp.dot(x, wu_v[cols(j)], preferred_element_type=F32),
        )

    zero = jnp.zeros((batch, wg_v.shape[1]), F32)
    gate, up = lax.fori_loop(0, chunks, hidden_units, (zero, zero))
    act = (gate / (1.0 + jnp.exp(-gate)) * up).astype(BF16)

    @pl.loop(0, chunks)
    def _(step):
        j = turn(step)
        load_wd(j).wait()
        term = jnp.dot(act, big_v[j], preferred_element_type=F32)
        send_chunk(j, term, fs_send, fs_all, fs_ss, fs_rs)

    fs_all[me] = fs_send[me]
    receive_all(fs_send, fs_all, fs_ss, fs_rs)
    total = hid_s[me]
    for s in range(count):
        total = total + fs_all[s].astype(F32)
    out_ref[...] = total.astype(BF16)

    for d in range(1, groups):
        exchange(d, q_send, q_all, q_ss, q_rs, True).wait_send()
        exchange(d, log_send, log_all, log_ss, log_rs, True).wait_send()
        exchange(d, part_send, part_all, part_ss, part_rs, True).wait_send()
    sent_all(rs_send, rs_all, rs_ss, rs_rs)
    sent_all(ag_send, ag_all, ag_ss, ag_rs)
    sent_all(fs_send, fs_all, fs_ss, fs_rs)


def per_device(*operands):
    (hidden_in, queries_nope, queries_rope, cache, lengths, w_uk, w_uv, w_out, norm_gain,
     w_gate, w_up, w_down) = operands
    groups, tps = lax.axis_size("kvp"), lax.axis_size("tp")
    count = groups * tps
    batch, heads, head_dim = queries_nope.shape
    latent, rope, ctx = w_uk.shape[2], queries_rope.shape[2], cache.shape[1]
    width = hidden_in.shape[1]
    share = width // count
    ff = w_gate.shape[1]
    rows = w_out.shape[0]
    per_chunk = 1
    while share * per_chunk % 128 and per_chunk < count:
        per_chunk *= 2
    chunk = share * per_chunk
    held = (w_gate.size + w_up.size + max(rows, ff) * width + cache.size + w_uk.size + w_uv.size) * 2
    fits = (
        batch % 8 == 0
        and heads % 8 == 0
        and all(size % 128 == 0 for size in (head_dim, latent, ctx, chunk, ff))
        and count % per_chunk == 0
        and rows <= ff
        and held < VMEM_BYTES - 8 * 2**20
    )
    if not fits:
        return plain_device(*operands)
    chunks = width // chunk
    dma = pltpu.SemaphoreType.DMA
    vmem = pl.BlockSpec(memory_space=pltpu.VMEM)
    anywhere = pl.BlockSpec(memory_space=pl.ANY)
    spread = pltpu.VMEM((count, batch, share), BF16)
    scratch = [
        pltpu.VMEM((batch, latent + rope, ctx), BF16),
        pltpu.VMEM(w_uk.shape, BF16),
        pltpu.VMEM(w_uv.shape, BF16),
        pltpu.VMEM((chunks, ff, chunk), BF16),
        pltpu.VMEM(w_gate.shape, BF16),
        pltpu.VMEM(w_up.shape, BF16),
        pltpu.VMEM((batch, heads, head_dim), F32),
        pltpu.VMEM((batch, heads, latent), F32),
        pltpu.VMEM((batch, heads, latent + rope), BF16),
        pltpu.VMEM((groups, batch, heads, latent + rope), BF16),
        pltpu.VMEM((batch, groups * heads, ctx), F32),
        pltpu.VMEM((groups, batch, heads, latent), BF16),
        pltpu.VMEM((groups, batch, heads, latent), BF16),
        pltpu.VMEM((groups, batch, heads, 128), F32),
        pltpu.VMEM((groups, batch, heads, 128), F32),
        pltpu.VMEM((batch, heads, latent), F32),
        pltpu.VMEM((batch, heads * head_dim), BF16),
        pltpu.VMEM((count, batch, share), F32),
        spread,
        spread,
        pltpu.VMEM((batch, share), BF16),
        spread,
        pltpu.VMEM((batch, width), F32),
        pltpu.VMEM((batch, width), BF16),
        spread,
        spread,
        dma, dma, dma,
        dma((chunks,)), dma((chunks,)), dma((chunks,)), dma((chunks,)),
    ] + [dma((groups,))] * 6 + [dma((count,))] * 6
    return pl.pallas_call(
        functools.partial(layer_kernel, groups, tps, share, chunk, rows),
        out_shape=jax.ShapeDtypeStruct((batch, share), BF16),
        in_specs=[vmem, vmem, vmem, pl.BlockSpec(memory_space=pltpu.SMEM), vmem] + [anywhere] * 7,
        out_specs=vmem,
        scratch_shapes=scratch,
        compiler_params=pltpu.CompilerParams(
            collective_id=0, has_side_effects=True, vmem_limit_bytes=VMEM_BYTES
        ),
    )(
        hidden_in, queries_nope, queries_rope, lengths, norm_gain.reshape(1, width),
        jnp.swapaxes(cache, 1, 2), w_uk, w_uv, w_out, w_gate, w_up, w_down,
    )


def solution(mesh):
    placed = (
        P("grp", None),
        P("grp", ("kvp", "tp"), None),
        P("grp", ("kvp", "tp"), None),
        P("grp", "kvp", None),
        P("grp"),
        P(("kvp", "tp"), None, None),
        P(("kvp", "tp"), None, None),
        P(("kvp", "tp"), None),
        P(),
        P(None, ("kvp", "tp")),
        P(None, ("kvp", "tp")),
        P(("kvp", "tp"), None),
    )
    return jax.shard_map(
        per_device, mesh=mesh, in_specs=placed, out_specs=P("grp", ("kvp", "tp")), check_vma=False
    )
```

profile of v0, /device:TPU:0, one launch (start us, length us, event | category | flops | bytes accessed | tf_op | source)
XLA Modules:
  0.0 46.1 jit_solution(650407084910625536)
XLA Ops:
  0.0 44.8 %shard_map.118 = bf16[8,448]{1,0:T(8,128)(2,1)} custom-call(bf16[8,7168]{1,0:T(8,128)(2,1)} %hidden_ref.1, bf16[8,8,128]{2,1,0:T(8,128)(2,1)} %nope_ref.1, bf16[8,8,64]{2,1,0:T(8,128)(2,1)} %rope_ref.1, s32[8]{0:T(128)} %len_ref.1, f32[1,7168]{1,0:T(1,128)} %bitcast.3, bf16[8,576,384]{2,1,0:T(8,128)(2,1)} %bitcast.2, bf16[8,128,512]{2,1,0:T(8,128)(2,1)} %uk_hbm.1, ...), custom_call_target="tpu_custom_call" | custom-call | tf_op jit(solution)/shard_map/pallas_call | solution.py:425
  44.8 1.3 %copy.14 = bf16[8,448]{1,0:T(8,128)(2,1)} copy(bf16[8,448]{1,0:T(8,128)(2,1)} %shard_map.118) | data formatting | bytes 14336
where the time goes:
time: 46.3 us; the launch traced here: 46.1 us
  Pallas kernels  44.8 us (97%)
  local copies, waits for them, and re-layouts  1.3 us (3%)
    pallas_call x1, Pallas kernels, per_device(): pl.pallas_call(functools.partial(layer_kernel, groups, tps, share, chunk,...  44.8 us
    unnamed x1, local copies, waits for them, and re-layouts  1.3 us

commit v1 on v0

v1 whole, which is shorter than its diff:
```python
import functools

import jax
import jax.numpy as jnp
from jax import lax
from jax.experimental import pallas as pl
from jax.experimental.pallas import tpu as pltpu
from jax.sharding import PartitionSpec as P


def project(o_lat, w_uv, w_out):
    head_out = jnp.einsum("bhl,hle->bhe", o_lat, w_uv, preferred_element_type=jnp.float32).astype(
        jnp.bfloat16
    )
    return jnp.dot(
        head_out.reshape(head_out.shape[0], -1), w_out, preferred_element_type=jnp.float32
    )


def plain_device(
    hidden_in,
    queries_nope,
    queries_rope,
    cache,
    lengths,
    w_uk,
    w_uv,
    w_out,
    norm_gain,
    w_gate,
    w_up,
    w_down,
):
    batch, heads_dev, head_dim = queries_nope.shape
    latent = w_uk.shape[2]
    ctx_dev = cache.shape[1]
    groups = lax.axis_size("kvp")
    score_scale = float(head_dim + queries_rope.shape[2]) ** (-0.5)
    q_lat = jnp.einsum(
        "bhd,hdl->bhl", queries_nope, w_uk, preferred_element_type=jnp.float32
    ).astype(jnp.bfloat16)
    q_lat_all, rope_all = (
        lax.all_gather(q_lat, "kvp", axis=1, tiled=True),
        lax.all_gather(queries_rope, "kvp", axis=1, tiled=True),
    )
    q_full = jnp.concatenate([q_lat_all, rope_all], axis=2)
    scores = (
        jnp.einsum("bhc,btc->bht", q_full, cache, preferred_element_type=jnp.float32) * score_scale
    )
    offset = lax.axis_index("kvp") * ctx_dev
    visible = ((offset + jnp.arange(ctx_dev, dtype=jnp.int32))[None, :] < lengths[:, None])[
        :, None, :
    ]
    masked = jnp.where(visible, scores, jnp.float32(-1e30))
    block_max = jnp.max(masked, axis=2)
    exponent = jnp.where(visible, jnp.exp(masked - block_max[..., None]), jnp.float32(0.0))
    guarded = jnp.maximum(jnp.sum(exponent, axis=2), 1.0)
    log_total = block_max + jnp.log(guarded)
    weights = (exponent / guarded[..., None]).astype(jnp.bfloat16)
    partial_value = jnp.einsum("bht,btc->bhc", weights, cache, preferred_element_type=jnp.float32)[
        ..., :latent
    ]
    blocks = partial_value.reshape(batch, groups, heads_dev, latent)
    block_logs = log_total.reshape(batch, groups, heads_dev)
    part_blocks = lax.all_to_all(
        blocks.astype(jnp.bfloat16), "kvp", split_axis=1, concat_axis=1, tiled=True
    ).astype(blocks.dtype)
    part_logs = lax.all_to_all(block_logs, "kvp", split_axis=1, concat_axis=1, tiled=True)
    highest = jnp.max(part_logs, axis=1)
    overall = highest + jnp.log(jnp.sum(jnp.exp(part_logs - highest[:, None, :]), axis=1))
    scaled = jnp.exp(part_logs - overall[:, None, :])[..., None] * part_blocks
    o_lat = jnp.sum(scaled, axis=1).astype(jnp.bfloat16)
    attention = project(o_lat, w_uv, w_out)
    model_width = norm_gain.shape[0]
    share_width = model_width // lax.axis_size(("kvp", "tp"))
    share_start = lax.axis_index(("kvp", "tp")) * share_width
    attn_whole = lax.psum(attention, ("kvp", "tp"))
    residual = hidden_in.astype(jnp.float32) + attn_whole
    mean_square = jnp.mean(residual * residual, axis=1)
    normed = (residual * lax.rsqrt(mean_square + 1e-06)[:, None] * norm_gain[None, :]).astype(
        jnp.bfloat16
    )
    residual_share = lax.dynamic_slice_in_dim(residual, share_start, share_width, 1)
    gate_proj = jnp.dot(normed, w_gate, preferred_element_type=jnp.float32)
    up_proj = jnp.dot(normed, w_up, preferred_element_type=jnp.float32)
    act = (jax.nn.silu(gate_proj) * up_proj).astype(jnp.bfloat16)
    ffn_terms = jnp.dot(act, w_down, preferred_element_type=jnp.float32)
    ffn_share = lax.psum_scatter(ffn_terms, ("kvp", "tp"), scatter_dimension=1, tiled=True)
    return (residual_share + ffn_share).astype(jnp.bfloat16)


MESH = pl.DeviceIdType.MESH
F32 = jnp.float32
BF16 = jnp.bfloat16
VMEM_BYTES = 67043328


SPAN = 4


def layer_kernel(
    groups, tps, share, chunk, out_rows, span,
    hidden_hbm, nope_hbm, rope_hbm, len_hbm, gain_hbm,
    cache_hbm, uk_hbm, uv_hbm, wo_hbm, wg_hbm, wu_hbm, wd_hbm,
    out_ref,
    hidden_v, nope_v, rope_v, len_v, gain_v, gain_s,
    cache_v, uk_v, uv_v, big_v, gu_v,
    nope_s, qlat_s, score_s, weight_s, q_send, q_all, part_send, part_all, log_send, log_all,
    olat_s, head_s, own_s, rs_send, rs_all, ag_send, ag_all, fs_send, fs_all,
    in_sem, uk_sem, cache_sem, uv_sem, wo_sem, gu_sem, wd_sem,
    q_ss, q_rs, part_ss, part_rs, log_ss, log_rs, rs_ss, rs_rs, ag_ss, ag_rs, fs_ss, fs_rs,
):
    count = groups * tps
    kvp = lax.axis_index("kvp")
    tp = lax.axis_index("tp")
    me = kvp * tps + tp
    batch, heads, head_dim = nope_v.shape
    latent = uk_v.shape[2]
    rope = rope_v.shape[2]
    ctx = cache_v.shape[2]
    width = hidden_v.shape[1]
    chunks = width // chunk
    hidden_units = gu_v.shape[1] // 2
    parts = batch // span
    halves = tps // 2
    half = tp // 2
    chips = groups // 2

    def peer(index):
        return {"kvp": index // tps, "tp": lax.rem(index, tps)}

    def target_of(i):
        return lax.rem(kvp // 2 + i // 2, chips) * 2 + lax.rem(kvp + i, 2)

    def source_of(i):
        return lax.rem(kvp // 2 + chips - i // 2, chips) * 2 + lax.rem(kvp + i, 2)

    def owner_tp(h):
        return 2 * h + 1 - (4 * h + 2) // tps

    near = [
        (target_of(i), lax.rem(half + e, halves)) for e in range(halves) for i in range(groups)
    ]
    far = near[::-1]
    mine = kvp * halves + half
    owns = tp == owner_tp(half)

    def load(source, target, sem):
        return pltpu.make_async_copy(source, target, sem)

    def cols(j):
        return pl.ds(pl.multiple_of(j * chunk, 128), chunk)

    def side(t):
        return pl.ds((t % 2) * chunk, chunk)

    def load_wo(t):
        k, h = far[t]
        return load(
            wo_hbm.at[:, cols(k * halves + h)],
            big_v.at[t // 2, pl.ds(0, out_rows), side(t)],
            wo_sem.at[t],
        )

    def load_wd(t):
        k, h = far[t]
        return load(wd_hbm.at[:, cols(k * halves + h)], big_v.at[t // 2, :, side(t)], wd_sem.at[t])

    def load_gu(t, n):
        k, h = near[t]
        return load(
            (wg_hbm, wu_hbm)[n].at[cols(k * halves + h)],
            gu_v.at[pl.ds(t * chunk, chunk), pl.ds(n * hidden_units, hidden_units)],
            gu_sem.at[n, t],
        )

    small = [
        load(nope_hbm, nope_v, in_sem.at[0]),
        load(rope_hbm, rope_v, in_sem.at[1]),
        load(len_hbm, len_v, in_sem.at[2]),
        load(hidden_hbm, hidden_v, in_sem.at[3]),
        load(gain_hbm, gain_v.at[:, pl.ds(0, width)], in_sem.at[4]),
    ]
    uk_load = load(uk_hbm, uk_v, uk_sem)
    cache_load = load(cache_hbm, cache_v, cache_sem)
    uv_load = load(uv_hbm, uv_v, uv_sem)

    barrier = pltpu.get_barrier_semaphore()
    small[0].start()
    uk_load.start()
    small[1].start()

    @pl.loop(1, count)
    def _(d):
        pl.semaphore_signal(
            barrier, inc=1, device_id=peer(lax.rem(me + d, count)), device_id_type=MESH
        )

    cache_load.start()
    for copy in small[2:]:
        copy.start()

    small[0].wait()
    nope_s[...] = nope_v[...].astype(F32)
    small[1].wait()
    base = 2 * latent
    for b in range(batch):
        first = base + (b % 2) * rope
        q_send[b // 2, :, first : first + rope] = rope_v[b]
    uk_load.wait()
    for i in range(heads):
        qlat_s[:, i, :] = jnp.dot(
            nope_s[:, i, :].astype(BF16), uk_v[i], preferred_element_type=F32
        )
    for b in range(batch):
        first = (b % 2) * latent
        q_send[b // 2, :, first : first + latent] = qlat_s[b].astype(BF16)
    pl.semaphore_wait(barrier, count - 1)

    def q_copy(i, u, ahead):
        other = target_of(i) if ahead else source_of(i)
        return pltpu.make_async_remote_copy(
            src_ref=q_send.at[pl.ds(u * span // 2, span // 2)],
            dst_ref=q_all.at[kvp if ahead else other, pl.ds(u * span // 2, span // 2)],
            send_sem=q_ss.at[i, u],
            recv_sem=q_rs.at[kvp if ahead else other, u],
            device_id={"kvp": other, "tp": tp},
            device_id_type=MESH,
        )

    def part_copy(i, u, ahead):
        other = target_of(i) if ahead else source_of(i)
        slot = kvp if ahead else other
        some = pl.ds(u * span, span)
        return pltpu.make_async_remote_copy(
            src_ref=part_send.at[other, some],
            dst_ref=part_all.at[slot, some],
            send_sem=part_ss.at[i, u],
            recv_sem=part_rs.at[slot, u],
            device_id={"kvp": other, "tp": tp},
            device_id_type=MESH,
        )

    def log_copy(i, ahead):
        other = target_of(i) if ahead else source_of(i)
        slot = kvp if ahead else other
        return pltpu.make_async_remote_copy(
            src_ref=log_send.at[other],
            dst_ref=log_all.at[slot],
            send_sem=log_ss.at[i],
            recv_sem=log_rs.at[slot],
            device_id={"kvp": other, "tp": tp},
            device_id_type=MESH,
        )

    outward = list(range(2, groups)) + [1]
    for u in range(parts):
        for i in outward:
            q_copy(i, u, True).start()
    uv_load.start(priority=1)
    for t in range(chunks):
        load_wo(t).start(priority=1)
    for t in range(chunks):
        load_gu(t, 0).start(priority=1)
        load_gu(t, 1).start(priority=1)
    q_all[kvp] = q_send[...]
    for copy in small[2:]:
        copy.wait()
    for j in range(chunks):
        gain_s[j] = jnp.broadcast_to(gain_v[:, j * chunk : (j + 1) * chunk], (batch, chunk))
    cache_load.wait()

    scale = float(head_dim + rope) ** (-0.5)
    rows = groups * heads
    position = kvp * ctx + lax.broadcasted_iota(jnp.int32, (rows, ctx), 1)
    lane = lax.broadcasted_iota(jnp.int32, (rows, 128), 1)
    logs_acc = jnp.zeros((rows, 128), F32)
    lengths = len_v[...]
    for u in range(parts):
        for i in range(1, groups):
            q_copy(i, u, False).wait_recv()
        some = range(u * span, (u + 1) * span)
        for b in some:
            lat = (b % 2) * latent
            rot = base + (b % 2) * rope
            q_lat = q_all[:, b // 2, :, lat : lat + latent].astype(F32).reshape(rows, latent)
            q_rot = q_all[:, b // 2, :, rot : rot + rope].astype(F32).reshape(rows, rope)
            score_s[b] = (
                jnp.dot(q_lat.astype(BF16), cache_v[b, :latent], preferred_element_type=F32)
                + jnp.dot(q_rot.astype(BF16), cache_v[b, latent:], preferred_element_type=F32)
            ) * scale
        for b in some:
            visible = position < lengths[:, b : b + 1]
            masked = jnp.where(visible, score_s[b], F32(-1e30))
            top = jnp.max(masked, axis=1, keepdims=True)
            exps = jnp.where(visible, jnp.exp(masked - top), F32(0.0))
            guarded = jnp.maximum(jnp.sum(exps, axis=1, keepdims=True), 1.0)
            logs_acc = jnp.where(lane == b, top + jnp.log(guarded), logs_acc)
            weight_s[b] = (exps / guarded).astype(BF16)
        for b in some:
            part = lax.dot_general(
                weight_s[b], cache_v[b, :latent], (((1,), (1,)), ((), ())),
                preferred_element_type=F32,
            )
            for g in range(groups):
                part_send[g, b] = part[g * heads : (g + 1) * heads].astype(BF16)
        for i in outward:
            part_copy(i, u, True).start()
    for g in range(groups):
        log_send[g] = logs_acc[g * heads : (g + 1) * heads]
    for i in outward:
        log_copy(i, True).start()
    part_all[kvp] = part_send[kvp]
    log_all[kvp] = log_send[kvp]
    uv_load.wait()
    for t in range(chunks):
        load_wo(t).wait()
    for i in range(1, groups):
        log_copy(i, False).wait_recv()
    logs = [log_all[g] for g in range(groups)]
    highest = functools.reduce(jnp.maximum, logs)
    overall = highest + jnp.log(sum(jnp.exp(x - highest) for x in logs))
    factors = [jnp.exp(x - overall) for x in logs]
    for u in range(parts):
        for i in range(1, groups):
            part_copy(i, u, False).wait_recv()
        for b in range(u * span, (u + 1) * span):
            olat_s[b] = sum(
                factors[g][:, b : b + 1] * part_all[g, b].astype(F32) for g in range(groups)
            )
    for i in range(heads):
        head_s[:, i * head_dim : (i + 1) * head_dim] = jnp.dot(
            olat_s[:, i, :].astype(BF16), uv_v[i], preferred_element_type=F32
        ).astype(BF16)

    def rs_copy(t, slot, k, z):
        return pltpu.make_async_remote_copy(
            src_ref=rs_send.at[t],
            dst_ref=rs_all.at[slot],
            send_sem=rs_ss.at[t],
            recv_sem=rs_rs.at[slot],
            device_id={"kvp": k, "tp": z},
            device_id_type=MESH,
        )

    for s in range(chunks // 2):
        both = jnp.dot(head_s[...], big_v[s, :out_rows], preferred_element_type=F32)
        for t in (2 * s, 2 * s + 1):
            k, h = far[t]
            load_wd(t).start(priority=1)
            term = both[:, (t % 2) * chunk : (t % 2 + 1) * chunk]
            rs_send[t] = term.astype(BF16)
            if t < chunks - 1:
                rs_copy(t, me, k, owner_tp(h)).start()
            else:
                own_s[...] = term

                @pl.when(jnp.logical_not(owns))
                def _():
                    rs_copy(t, me, k, owner_tp(h)).start()

    def ag_copy(d, slot, dest):
        return pltpu.make_async_remote_copy(
            src_ref=ag_send,
            dst_ref=ag_all.at[slot],
            send_sem=ag_ss.at[d],
            recv_sem=ag_rs.at[slot],
            device_id=peer(dest),
            device_id_type=MESH,
        )

    @pl.when(owns)
    def _():
        residual = hidden_v[:, cols(mine)].astype(F32) + own_s[...]
        for d in range(1, count):
            source = lax.rem(me + d, count)
            rs_copy(0, source, source // tps, lax.rem(source, tps)).wait_recv()
        total = residual
        for d in range(1, count):
            total = total + rs_all[lax.rem(me + d, count)].astype(F32)
        ag_send[...] = total.astype(BF16)

        @pl.loop(1, count)
        def _(d):
            ag_copy(d, mine, lax.rem(me + d, count)).start()

        ag_all[mine] = ag_send[...]

    square = jnp.zeros((batch, 1), F32)
    for t in range(chunks):
        load_gu(t, 0).wait()
        load_gu(t, 1).wait()
    products = jnp.zeros((batch, 2 * hidden_units), F32)
    for s in range(chunks // 2):
        x = []
        for t in (2 * s, 2 * s + 1):
            k, h = near[t]
            j = k * halves + h
            if t == 0:
                @pl.when(jnp.logical_not(owns))
                def _():
                    ag_copy(0, j, k * tps + owner_tp(h)).wait_recv()
            else:
                ag_copy(0, j, k * tps + owner_tp(h)).wait_recv()
        for t in (2 * s, 2 * s + 1):
            k, h = near[t]
            j = k * halves + h
            value = ag_all[j].astype(F32)
            square = square + jnp.sum(value * value, axis=1, keepdims=True)
            x.append((value * gain_s[j]).astype(BF16))
        products = products + jnp.dot(
            jnp.concatenate(x, axis=1),
            gu_v[2 * s * chunk : 2 * (s + 1) * chunk],
            preferred_element_type=F32,
        )
    products = products * lax.rsqrt(square / width + 1e-06)
    gate, up = products[:, :hidden_units], products[:, hidden_units:]
    act = (gate / (1.0 + jnp.exp(-gate)) * up).astype(BF16)

    def fs_copy(n, slot, k, z):
        return pltpu.make_async_remote_copy(
            src_ref=fs_send.at[n],
            dst_ref=fs_all.at[slot],
            send_sem=fs_ss.at[n],
            recv_sem=fs_rs.at[slot],
            device_id={"kvp": k, "tp": z},
            device_id_type=MESH,
        )

    pair = ag_all[mine].astype(F32)
    total = jnp.where(lax.rem(tp, 2) == 0, pair[:, :share], pair[:, share:])
    for t in range(chunks):
        load_wd(t).wait()
    for s in range(chunks // 2):
        both = jnp.dot(act, big_v[s], preferred_element_type=F32)
        for n in range(4 * s, 4 * s + 4):
            k, h = far[n // 2]
            p = n % 2
            piece = both[:, (n % 4) * share : (n % 4 + 1) * share]
            fs_send[n] = piece.astype(BF16)
            if n < count - 2:
                fs_copy(n, me, k, 2 * h + p).start()
            else:
                total = total + jnp.where(lax.rem(tp, 2) == p, piece, F32(0.0))

                @pl.when(lax.rem(tp, 2) != p)
                def _():
                    fs_copy(n, me, k, 2 * h + p).start()

    for d in range(1, count):
        source = lax.rem(me + d, count)
        fs_copy(0, source, source // tps, lax.rem(source, tps)).wait_recv()
    for d in range(1, count):
        total = total + fs_all[lax.rem(me + d, count)].astype(F32)
    out_ref[...] = total.astype(BF16)

    for i in range(1, groups):
        for u in range(parts):
            q_copy(i, u, True).wait_send()
            part_copy(i, u, True).wait_send()
        log_copy(i, True).wait_send()
    for t, (k, h) in enumerate(far):
        if t < chunks - 1:
            rs_copy(t, me, k, owner_tp(h)).wait_send()
            fs_copy(2 * t, me, k, 2 * h).wait_send()
            fs_copy(2 * t + 1, me, k, 2 * h + 1).wait_send()
        else:
            @pl.when(jnp.logical_not(owns))
            def _():
                rs_copy(t, me, k, owner_tp(h)).wait_send()

            for p in range(2):
                @pl.when(lax.rem(tp, 2) != p)
                def _():
                    fs_copy(2 * t + p, me, k, 2 * h + p).wait_send()

    @pl.when(owns)
    def _():
        @pl.loop(1, count)
        def _(d):
            ag_copy(d, mine, lax.rem(me + d, count)).wait_send()


def per_device(*operands):
    (hidden_in, queries_nope, queries_rope, cache, lengths, w_uk, w_uv, w_out, norm_gain,
     w_gate, w_up, w_down) = operands
    groups, tps = lax.axis_size("kvp"), lax.axis_size("tp")
    count = groups * tps
    batch, heads, head_dim = queries_nope.shape
    latent, rope, ctx = w_uk.shape[2], queries_rope.shape[2], cache.shape[1]
    width = hidden_in.shape[1]
    share = width // count
    ff = w_gate.shape[1]
    rows = w_out.shape[0]
    chunk = 2 * share
    held = (w_gate.size + w_up.size + max(rows, ff) * width + cache.size + w_uk.size + w_uv.size) * 2
    fits = (
        batch % 8 == 0
        and heads % 8 == 0
        and all(size % 128 == 0 for size in (head_dim, latent, 2 * rope, ctx, chunk, ff))
        and groups % 2 == 0
        and tps % 2 == 0
        and batch <= 128
        and rows <= ff
        and held < VMEM_BYTES - 8 * 2**20
    )
    if not fits:
        return plain_device(*operands)
    chunks = width // chunk
    pairs = batch // 2
    parts = batch // SPAN
    dma = pltpu.SemaphoreType.DMA
    vmem = pl.BlockSpec(memory_space=pltpu.VMEM)
    anywhere = pl.BlockSpec(memory_space=pl.ANY)
    packed = 2 * (latent + rope)
    scratch = [
        pltpu.VMEM((batch, width), BF16),
        pltpu.VMEM((batch, heads, head_dim), BF16),
        pltpu.VMEM((batch, heads, rope), BF16),
        pltpu.VMEM((1, batch), jnp.int32),
        pltpu.VMEM((1, width + 1024), F32),
        pltpu.VMEM((chunks, batch, chunk), F32),
        pltpu.VMEM((batch, latent + rope, ctx), BF16),
        pltpu.VMEM(w_uk.shape, BF16),
        pltpu.VMEM(w_uv.shape, BF16),
        pltpu.VMEM((chunks // 2, ff, 2 * chunk), BF16),
        pltpu.VMEM((width, 2 * ff), BF16),
        pltpu.VMEM((batch, heads, head_dim), F32),
        pltpu.VMEM((batch, heads, latent), F32),
        pltpu.VMEM((batch, groups * heads, ctx), F32),
        pltpu.VMEM((batch, groups * heads, ctx), BF16),
        pltpu.VMEM((pairs, heads, packed), BF16),
        pltpu.VMEM((groups, pairs, heads, packed), BF16),
        pltpu.VMEM((groups, batch, heads, latent), BF16),
        pltpu.VMEM((groups, batch, heads, latent), BF16),
        pltpu.VMEM((groups, heads, 128), F32),
        pltpu.VMEM((groups, heads, 128), F32),
        pltpu.VMEM((batch, heads, latent), F32),
        pltpu.VMEM((batch, heads * head_dim), BF16),
        pltpu.VMEM((batch, chunk), F32),
        pltpu.VMEM((chunks, batch, chunk), BF16),
        pltpu.VMEM((count, batch, chunk), BF16),
        pltpu.VMEM((batch, chunk), BF16),
        pltpu.VMEM((chunks, batch, chunk), BF16),
        pltpu.VMEM((count, batch, share), BF16),
        pltpu.VMEM((count, batch, share), BF16),
        dma((5,)), dma, dma, dma,
        dma((chunks,)), dma((2, chunks)), dma((chunks,)),
        dma((groups, parts)), dma((groups, parts)), dma((groups, parts)), dma((groups, parts)),
        dma((groups,)), dma((groups,)),
        dma((chunks,)), dma((count,)), dma((count,)), dma((chunks,)), dma((count,)), dma((count,)),
    ]
    return pl.pallas_call(
        functools.partial(layer_kernel, groups, tps, share, chunk, rows, SPAN),
        out_shape=jax.ShapeDtypeStruct((batch, share), BF16),
        in_specs=[anywhere] * 12,
        out_specs=vmem,
        scratch_shapes=scratch,
        compiler_params=pltpu.CompilerParams(
            collective_id=0, has_side_effects=True, vmem_limit_bytes=VMEM_BYTES
        ),
    )(
        hidden_in, queries_nope, queries_rope, lengths.reshape(1, batch), norm_gain.reshape(1, width),
        jnp.swapaxes(cache, 1, 2), w_uk, w_uv, w_out, w_gate, w_up, w_down,
    )


def solution(mesh):
    placed = (
        P("grp", None),
        P("grp", ("kvp", "tp"), None),
        P("grp", ("kvp", "tp"), None),
        P("grp", "kvp", None),
        P("grp"),
        P(("kvp", "tp"), None, None),
        P(("kvp", "tp"), None, None),
        P(("kvp", "tp"), None),
        P(),
        P(None, ("kvp", "tp")),
        P(None, ("kvp", "tp")),
        P(("kvp", "tp"), None),
    )
    return jax.shard_map(
        per_device, mesh=mesh, in_specs=placed, out_specs=P("grp", ("kvp", "tp")), check_vma=False
    )
```

time: 46.3 us -> 44.4 us (0.959)
  Pallas kernels: 44.8 us -> 42.8 us
    pallas_call x1, Pallas kernels: 44.8 us -> 42.8 us  [per_device(): pl.pallas_call(functools.partial(layer_kernel, groups, tps, share, chunk,...]
where the time goes in v1:
time: 44.4 us; the launch traced here: 44.2 us
  Pallas kernels  42.8 us (96%)
  local copies, waits for them, and re-layouts  1.3 us (3%)
    pallas_call x1, Pallas kernels, per_device(): pl.pallas_call(functools.partial(layer_kernel, groups, tps, share, chunk,...  42.8 us
    unnamed x1, local copies, waits for them, and re-layouts  1.3 us

profile of v1, /device:TPU:0, one launch (start us, length us, event | category | flops | bytes accessed | tf_op | source)
XLA Modules:
  0.0 44.2 jit_solution(7098830095655554733)
XLA Ops:
  0.0 42.8 %shard_map.118 = bf16[8,448]{1,0:T(8,128)(2,1)} custom-call(bf16[8,7168]{1,0:T(8,128)(2,1)} %hidden_hbm.1, bf16[8,8,128]{2,1,0:T(8,128)(2,1)} %nope_hbm.1, bf16[8,8,64]{2,1,0:T(8,128)(2,1)} %rope_hbm.1, s32[1,8]{1,0:T(1,128)} %bitcast.5, f32[1,7168]{1,0:T(1,128)} %bitcast.4, bf16[8,576,384]{2,1,0:T(8,128)(2,1)} %bitcast.3, bf16[8,128,512]{2,1,0:T(8,128)(2,1)} %uk_hbm.1, ...), custom_call_target="tpu_custom_call" | custom-call | tf_op jit(solution)/shard_map/pallas_call | solution.py:553
  42.9 1.3 %copy.14 = bf16[8,448]{1,0:T(8,128)(2,1)} copy(bf16[8,448]{1,0:T(8,128)(2,1)} %shard_map.118) | data formatting | bytes 14336

commit v2 on v1

--- a/solution.py
+++ b/solution.py
@@ -132,9 +132,6 @@
     def target_of(i):
         return lax.rem(kvp // 2 + i // 2, chips) * 2 + lax.rem(kvp + i, 2)
 
-    def source_of(i):
-        return lax.rem(kvp // 2 + chips - i // 2, chips) * 2 + lax.rem(kvp + i, 2)
-
     def owner_tp(h):
         return 2 * h + 1 - (4 * h + 2) // tps
 
@@ -159,20 +156,28 @@
         return load(
             wo_hbm.at[:, cols(k * halves + h)],
             big_v.at[t // 2, pl.ds(0, out_rows), side(t)],
-            wo_sem.at[t],
+            wo_sem,
         )
 
     def load_wd(t):
         k, h = far[t]
-        return load(wd_hbm.at[:, cols(k * halves + h)], big_v.at[t // 2, :, side(t)], wd_sem.at[t])
+        return load(wd_hbm.at[:, cols(k * halves + h)], big_v.at[t // 2, :, side(t)], wd_sem.at[2 * t // chunks])
 
     def load_gu(t, n):
         k, h = near[t]
         return load(
             (wg_hbm, wu_hbm)[n].at[cols(k * halves + h)],
             gu_v.at[pl.ds(t * chunk, chunk), pl.ds(n * hidden_units, hidden_units)],
-            gu_sem.at[n, t],
-        )
+            gu_sem.at[t // 2],
+        )
+
+    def landed(ref, sem):
+        pltpu.make_async_copy(ref, ref, sem).wait()
+
+    def load_step(s):
+        for t in (2 * s, 2 * s + 1):
+            load_gu(t, 0).start(priority=1)
+            load_gu(t, 1).start(priority=1)
 
     small = [
         load(nope_hbm, nope_v, in_sem.at[0]),
@@ -208,6 +213,9 @@
         first = base + (b % 2) * rope
         q_send[b // 2, :, first : first + rope] = rope_v[b]
     uk_load.wait()
+    uv_load.start()
+    for t in range(chunks):
+        load_wo(t).start()
     for i in range(heads):
         qlat_s[:, i, :] = jnp.dot(
             nope_s[:, i, :].astype(BF16), uk_v[i], preferred_element_type=F32
@@ -217,38 +225,36 @@
         q_send[b // 2, :, first : first + latent] = qlat_s[b].astype(BF16)
     pl.semaphore_wait(barrier, count - 1)
 
-    def q_copy(i, u, ahead):
-        other = target_of(i) if ahead else source_of(i)
+    def q_copy(i, u):
+        other = target_of(i)
         return pltpu.make_async_remote_copy(
             src_ref=q_send.at[pl.ds(u * span // 2, span // 2)],
-            dst_ref=q_all.at[kvp if ahead else other, pl.ds(u * span // 2, span // 2)],
-            send_sem=q_ss.at[i, u],
-            recv_sem=q_rs.at[kvp if ahead else other, u],
+            dst_ref=q_all.at[kvp, pl.ds(u * span // 2, span // 2)],
+            send_sem=q_ss,
+            recv_sem=q_rs.at[u],
             device_id={"kvp": other, "tp": tp},
             device_id_type=MESH,
         )
 
-    def part_copy(i, u, ahead):
-        other = target_of(i) if ahead else source_of(i)
-        slot = kvp if ahead else other
+    def part_copy(i, u):
+        other = target_of(i)
         some = pl.ds(u * span, span)
         return pltpu.make_async_remote_copy(
             src_ref=part_send.at[other, some],
-            dst_ref=part_all.at[slot, some],
-            send_sem=part_ss.at[i, u],
-            recv_sem=part_rs.at[slot, u],
+            dst_ref=part_all.at[kvp, some],
+            send_sem=part_ss,
+            recv_sem=part_rs.at[u],
             device_id={"kvp": other, "tp": tp},
             device_id_type=MESH,
         )
 
-    def log_copy(i, ahead):
-        other = target_of(i) if ahead else source_of(i)
-        slot = kvp if ahead else other
+    def log_copy(i):
+        other = target_of(i)
         return pltpu.make_async_remote_copy(
             src_ref=log_send.at[other],
-            dst_ref=log_all.at[slot],
-            send_sem=log_ss.at[i],
-            recv_sem=log_rs.at[slot],
+            dst_ref=log_all.at[kvp],
+            send_sem=log_ss,
+            recv_sem=log_rs,
             device_id={"kvp": other, "tp": tp},
             device_id_type=MESH,
         )
@@ -256,13 +262,10 @@
     outward = list(range(2, groups)) + [1]
     for u in range(parts):
         for i in outward:
-            q_copy(i, u, True).start()
-    uv_load.start(priority=1)
-    for t in range(chunks):
-        load_wo(t).start(priority=1)
-    for t in range(chunks):
-        load_gu(t, 0).start(priority=1)
-        load_gu(t, 1).start(priority=1)
+            q_copy(i, u).start()
+    steps = chunks // 2
+    for s in range(steps // 2):
+        load_step(s)
     q_all[kvp] = q_send[...]
     for copy in small[2:]:
         copy.wait()
@@ -277,8 +280,7 @@
     logs_acc = jnp.zeros((rows, 128), F32)
     lengths = len_v[...]
     for u in range(parts):
-        for i in range(1, groups):
-            q_copy(i, u, False).wait_recv()
+        landed(q_all.at[pl.ds(0, groups - 1), pl.ds(u * span // 2, span // 2)], q_rs.at[u])
         some = range(u * span, (u + 1) * span)
         for b in some:
             lat = (b % 2) * latent
@@ -305,25 +307,24 @@
             for g in range(groups):
                 part_send[g, b] = part[g * heads : (g + 1) * heads].astype(BF16)
         for i in outward:
-            part_copy(i, u, True).start()
+            part_copy(i, u).start()
     for g in range(groups):
         log_send[g] = logs_acc[g * heads : (g + 1) * heads]
     for i in outward:
-        log_copy(i, True).start()
+        log_copy(i).start()
+    for s in range(steps // 2, steps):
+        load_step(s)
     part_all[kvp] = part_send[kvp]
     log_all[kvp] = log_send[kvp]
     uv_load.wait()
-    for t in range(chunks):
-        load_wo(t).wait()
-    for i in range(1, groups):
-        log_copy(i, False).wait_recv()
+    landed(big_v.at[:, pl.ds(0, out_rows)], wo_sem)
+    landed(log_all.at[pl.ds(0, groups - 1)], log_rs)
     logs = [log_all[g] for g in range(groups)]
     highest = functools.reduce(jnp.maximum, logs)
     overall = highest + jnp.log(sum(jnp.exp(x - highest) for x in logs))
     factors = [jnp.exp(x - overall) for x in logs]
     for u in range(parts):
-        for i in range(1, groups):
-            part_copy(i, u, False).wait_recv()
+        landed(part_all.at[pl.ds(0, groups - 1), pl.ds(u * span, span)], part_rs.at[u])
         for b in range(u * span, (u + 1) * span):
             olat_s[b] = sum(
                 factors[g][:, b : b + 1] * part_all[g, b].astype(F32) for g in range(groups)
@@ -337,13 +338,13 @@
         return pltpu.make_async_remote_copy(
             src_ref=rs_send.at[t],
             dst_ref=rs_all.at[slot],
-            send_sem=rs_ss.at[t],
-            recv_sem=rs_rs.at[slot],
+            send_sem=rs_ss,
+            recv_sem=rs_rs,
             device_id={"kvp": k, "tp": z},
             device_id_type=MESH,
         )
 
-    for s in range(chunks // 2):
+    for s in range(steps):
         both = jnp.dot(head_s[...], big_v[s, :out_rows], preferred_element_type=F32)
         for t in (2 * s, 2 * s + 1):
             k, h = far[t]
@@ -363,7 +364,7 @@
         return pltpu.make_async_remote_copy(
             src_ref=ag_send,
             dst_ref=ag_all.at[slot],
-            send_sem=ag_ss.at[d],
+            send_sem=ag_ss,
             recv_sem=ag_rs.at[slot],
             device_id=peer(dest),
             device_id_type=MESH,
@@ -372,9 +373,7 @@
     @pl.when(owns)
     def _():
         residual = hidden_v[:, cols(mine)].astype(F32) + own_s[...]
-        for d in range(1, count):
-            source = lax.rem(me + d, count)
-            rs_copy(0, source, source // tps, lax.rem(source, tps)).wait_recv()
+        landed(rs_all.at[pl.ds(0, count - 1)], rs_rs)
         total = residual
         for d in range(1, count):
             total = total + rs_all[lax.rem(me + d, count)].astype(F32)
@@ -387,11 +386,10 @@
         ag_all[mine] = ag_send[...]
 
     square = jnp.zeros((batch, 1), F32)
-    for t in range(chunks):
-        load_gu(t, 0).wait()
-        load_gu(t, 1).wait()
+    for s in range(steps):
+        landed(gu_v.at[pl.ds(2 * s * chunk, 2 * chunk)], gu_sem.at[s])
     products = jnp.zeros((batch, 2 * hidden_units), F32)
-    for s in range(chunks // 2):
+    for s in range(steps):
         x = []
         for t in (2 * s, 2 * s + 1):
             k, h = near[t]
@@ -421,17 +419,17 @@
         return pltpu.make_async_remote_copy(
             src_ref=fs_send.at[n],
             dst_ref=fs_all.at[slot],
-            send_sem=fs_ss.at[n],
-            recv_sem=fs_rs.at[slot],
+            send_sem=fs_ss,
+            recv_sem=fs_rs,
             device_id={"kvp": k, "tp": z},
             device_id_type=MESH,
         )
 
     pair = ag_all[mine].astype(F32)
     total = jnp.where(lax.rem(tp, 2) == 0, pair[:, :share], pair[:, share:])
-    for t in range(chunks):
-        load_wd(t).wait()
-    for s in range(chunks // 2):
+    for s in range(2):
+        landed(big_v.at[pl.ds(s * steps // 2, steps // 2)], wd_sem.at[s])
+    for s in range(steps):
         both = jnp.dot(act, big_v[s], preferred_element_type=F32)
         for n in range(4 * s, 4 * s + 4):
             k, h = far[n // 2]
@@ -447,38 +445,25 @@
                 def _():
                     fs_copy(n, me, k, 2 * h + p).start()
 
-    for d in range(1, count):
-        source = lax.rem(me + d, count)
-        fs_copy(0, source, source // tps, lax.rem(source, tps)).wait_recv()
+    landed(fs_all.at[pl.ds(0, count - 1)], fs_rs)
     for d in range(1, count):
         total = total + fs_all[lax.rem(me + d, count)].astype(F32)
     out_ref[...] = total.astype(BF16)
 
-    for i in range(1, groups):
-        for u in range(parts):
-            q_copy(i, u, True).wait_send()
-            part_copy(i, u, True).wait_send()
-        log_copy(i, True).wait_send()
-    for t, (k, h) in enumerate(far):
-        if t < chunks - 1:
-            rs_copy(t, me, k, owner_tp(h)).wait_send()
-            fs_copy(2 * t, me, k, 2 * h).wait_send()
-            fs_copy(2 * t + 1, me, k, 2 * h + 1).wait_send()
-        else:
-            @pl.when(jnp.logical_not(owns))
-            def _():
-                rs_copy(t, me, k, owner_tp(h)).wait_send()
-
-            for p in range(2):
-                @pl.when(lax.rem(tp, 2) != p)
-                def _():
-                    fs_copy(2 * t + p, me, k, 2 * h + p).wait_send()
+    others = pl.ds(0, groups - 1)
+    landed(q_all.at[others], q_ss)
+    landed(part_all.at[others], part_ss)
+    landed(log_all.at[others], log_ss)
+    landed(fs_all.at[pl.ds(0, count - 1)], fs_ss)
 
     @pl.when(owns)
     def _():
-        @pl.loop(1, count)
-        def _(d):
-            ag_copy(d, mine, lax.rem(me + d, count)).wait_send()
+        landed(rs_all.at[pl.ds(0, chunks - 1)], rs_ss)
+        landed(rs_all.at[pl.ds(0, count - 1)], ag_ss)
+
+    @pl.when(jnp.logical_not(owns))
+    def _():
+        landed(rs_all.at[pl.ds(0, chunks)], rs_ss)
 
 
 def per_device(*operands):
@@ -499,7 +484,7 @@
         and heads % 8 == 0
         and all(size % 128 == 0 for size in (head_dim, latent, 2 * rope, ctx, chunk, ff))
         and groups % 2 == 0
-        and tps % 2 == 0
+        and tps % 4 == 0
         and batch <= 128
         and rows <= ff
         and held < VMEM_BYTES - 8 * 2**20
@@ -545,10 +530,9 @@
         pltpu.VMEM((count, batch, share), BF16),
         pltpu.VMEM((count, batch, share), BF16),
         dma((5,)), dma, dma, dma,
-        dma((chunks,)), dma((2, chunks)), dma((chunks,)),
-        dma((groups, parts)), dma((groups, parts)), dma((groups, parts)), dma((groups, parts)),
-        dma((groups,)), dma((groups,)),
-        dma((chunks,)), dma((count,)), dma((count,)), dma((chunks,)), dma((count,)), dma((count,)),
+        dma, dma((chunks // 2,)), dma((2,)),
+        dma, dma((parts,)), dma, dma((parts,)), dma, dma,
+        dma, dma, dma, dma((chunks,)), dma, dma,
     ]
     return pl.pallas_call(
         functools.partial(layer_kernel, groups, tps, share, chunk, rows, SPAN),

time: 44.4 us -> 38.8 us (0.87)
  Pallas kernels: 42.8 us -> 37.3 us
    pallas_call x1, Pallas kernels: 42.8 us -> 37.3 us  [per_device(): pl.pallas_call(functools.partial(layer_kernel, groups, tps, share, chunk,...]
where the time goes in v2:
time: 38.8 us; the launch traced here: 38.6 us
  Pallas kernels  37.3 us (96%)
  local copies, waits for them, and re-layouts  1.3 us (3%)
    pallas_call x1, Pallas kernels, per_device(): pl.pallas_call(functools.partial(layer_kernel, groups, tps, share, chunk,...  37.3 us
    unnamed x1, local copies, waits for them, and re-layouts  1.3 us

profile of v2, /device:TPU:0, one launch (start us, length us, event | category | flops | bytes accessed | tf_op | source)
XLA Modules:
  0.0 38.6 jit_solution(17576791113936025541)
XLA Ops:
  0.0 37.3 %shard_map.118 = bf16[8,448]{1,0:T(8,128)(2,1)} custom-call(bf16[8,7168]{1,0:T(8,128)(2,1)} %hidden_hbm.1, bf16[8,8,128]{2,1,0:T(8,128)(2,1)} %nope_hbm.1, bf16[8,8,64]{2,1,0:T(8,128)(2,1)} %rope_hbm.1, s32[1,8]{1,0:T(1,128)} %bitcast.5, f32[1,7168]{1,0:T(1,128)} %bitcast.4, bf16[8,576,384]{2,1,0:T(8,128)(2,1)} %bitcast.3, bf16[8,128,512]{2,1,0:T(8,128)(2,1)} %uk_hbm.1, ...), custom_call_target="tpu_custom_call" | custom-call | tf_op jit(solution)/shard_map/pallas_call | solution.py:537
  37.3 1.3 %copy.14 = bf16[8,448]{1,0:T(8,128)(2,1)} copy(bf16[8,448]{1,0:T(8,128)(2,1)} %shard_map.118) | data formatting | bytes 14336

commit v3 on v2

--- a/solution.py
+++ b/solution.py
@@ -95,7 +95,7 @@
 VMEM_BYTES = 67043328
 
 
-SPAN = 4
+SPAN = 2
 
 
 def layer_kernel(
@@ -106,9 +106,9 @@
     hidden_v, nope_v, rope_v, len_v, gain_v, gain_s,
     cache_v, uk_v, uv_v, big_v, gu_v,
     nope_s, qlat_s, score_s, weight_s, q_send, q_all, part_send, part_all, log_send, log_all,
-    olat_s, head_s, own_s, rs_send, rs_all, ag_send, ag_all, fs_send, fs_all,
+    olat_s, head_s, own_s, rp_send, rp_all, rs_send, rs_all, ag_send, ag_all, fp_send, fp_all, fs_send, fs_all,
     in_sem, uk_sem, cache_sem, uv_sem, wo_sem, gu_sem, wd_sem,
-    q_ss, q_rs, part_ss, part_rs, log_ss, log_rs, rs_ss, rs_rs, ag_ss, ag_rs, fs_ss, fs_rs,
+    q_ss, q_rs, part_ss, part_rs, log_ss, log_rs, rp_ss, rp_rs, rs_ss, rs_rs, ag_ss, ag_rs, fp_ss, fp_rs, fs_ss, fs_rs,
 ):
     count = groups * tps
     kvp = lax.axis_index("kvp")
@@ -138,7 +138,12 @@
     near = [
         (target_of(i), lax.rem(half + e, halves)) for e in range(halves) for i in range(groups)
     ]
-    far = near[::-1]
+    reach = [(e, i) for e in range(halves) for i in range(groups)][::-1]
+    order = [near[e * groups + i] for e, i in reach if i % 2 == 1]
+    order += [near[e * groups + i] for e, i in reach if i % 2 == 0]
+    sibling = {"kvp": target_of(1), "tp": tp}
+    sources = chips * tps
+    slot = (kvp // 2) * tps + tp
     mine = kvp * halves + half
     owns = tp == owner_tp(half)
 
@@ -152,7 +157,7 @@
         return pl.ds((t % 2) * chunk, chunk)
 
     def load_wo(t):
-        k, h = far[t]
+        k, h = order[t]
         return load(
             wo_hbm.at[:, cols(k * halves + h)],
             big_v.at[t // 2, pl.ds(0, out_rows), side(t)],
@@ -160,7 +165,7 @@
         )
 
     def load_wd(t):
-        k, h = far[t]
+        k, h = order[t]
         return load(wd_hbm.at[:, cols(k * halves + h)], big_v.at[t // 2, :, side(t)], wd_sem.at[2 * t // chunks])
 
     def load_gu(t, n):
@@ -334,38 +339,58 @@
             olat_s[:, i, :].astype(BF16), uv_v[i], preferred_element_type=F32
         ).astype(BF16)
 
-    def rs_copy(t, slot, k, z):
+    def pair_copy(b, source, target, ss, rs):
         return pltpu.make_async_remote_copy(
-            src_ref=rs_send.at[t],
+            src_ref=source.at[pl.ds(2 * b, 2)],
+            dst_ref=target.at[pl.ds(2 * b, 2)],
+            send_sem=ss,
+            recv_sem=rs.at[b],
+            device_id=sibling,
+            device_id_type=MESH,
+        )
+
+    def rs_copy(n, k, h):
+        return pltpu.make_async_remote_copy(
+            src_ref=rs_send.at[n],
             dst_ref=rs_all.at[slot],
             send_sem=rs_ss,
             recv_sem=rs_rs,
-            device_id={"kvp": k, "tp": z},
+            device_id={"kvp": k, "tp": owner_tp(h)},
             device_id_type=MESH,
         )
 
+    first_own = steps // 2
     for s in range(steps):
         both = jnp.dot(head_s[...], big_v[s, :out_rows], preferred_element_type=F32)
-        for t in (2 * s, 2 * s + 1):
-            k, h = far[t]
-            load_wd(t).start(priority=1)
-            term = both[:, (t % 2) * chunk : (t % 2 + 1) * chunk]
-            rs_send[t] = term.astype(BF16)
-            if t < chunks - 1:
-                rs_copy(t, me, k, owner_tp(h)).start()
-            else:
-                own_s[...] = term
-
-                @pl.when(jnp.logical_not(owns))
-                def _():
-                    rs_copy(t, me, k, owner_tp(h)).start()
-
-    def ag_copy(d, slot, dest):
+        load_wd(2 * s).start(priority=1)
+        load_wd(2 * s + 1).start(priority=1)
+        b = s % first_own
+        if s < first_own:
+            for q in range(2):
+                rp_send[2 * b + q] = both[:, q * chunk : (q + 1) * chunk].astype(BF16)
+            pair_copy(b, rp_send, rp_all, rp_ss, rp_rs).start()
+        else:
+            landed(rp_all.at[pl.ds(2 * b, 2)], rp_rs.at[b])
+            for q in range(2):
+                n = 2 * b + q
+                k, h = order[chunks // 2 + n]
+                term = both[:, q * chunk : (q + 1) * chunk] + rp_all[n].astype(F32)
+                rs_send[n] = term.astype(BF16)
+                if n < chunks // 2 - 1:
+                    rs_copy(n, k, h).start()
+                else:
+                    own_s[...] = term
+
+                    @pl.when(jnp.logical_not(owns))
+                    def _():
+                        rs_copy(n, k, h).start()
+
+    def ag_copy(d, j, dest):
         return pltpu.make_async_remote_copy(
             src_ref=ag_send,
-            dst_ref=ag_all.at[slot],
+            dst_ref=ag_all.at[j],
             send_sem=ag_ss,
-            recv_sem=ag_rs.at[slot],
+            recv_sem=ag_rs.at[j],
             device_id=peer(dest),
             device_id_type=MESH,
         )
@@ -373,10 +398,10 @@
     @pl.when(owns)
     def _():
         residual = hidden_v[:, cols(mine)].astype(F32) + own_s[...]
-        landed(rs_all.at[pl.ds(0, count - 1)], rs_rs)
+        landed(rs_all.at[pl.ds(0, sources - 1)], rs_rs)
         total = residual
-        for d in range(1, count):
-            total = total + rs_all[lax.rem(me + d, count)].astype(F32)
+        for d in range(1, sources):
+            total = total + rs_all[lax.rem(slot + d, sources)].astype(F32)
         ag_send[...] = total.astype(BF16)
 
         @pl.loop(1, count)
@@ -415,7 +440,7 @@
     gate, up = products[:, :hidden_units], products[:, hidden_units:]
     act = (gate / (1.0 + jnp.exp(-gate)) * up).astype(BF16)
 
-    def fs_copy(n, slot, k, z):
+    def fs_copy(n, k, z):
         return pltpu.make_async_remote_copy(
             src_ref=fs_send.at[n],
             dst_ref=fs_all.at[slot],
@@ -431,39 +456,51 @@
         landed(big_v.at[pl.ds(s * steps // 2, steps // 2)], wd_sem.at[s])
     for s in range(steps):
         both = jnp.dot(act, big_v[s], preferred_element_type=F32)
-        for n in range(4 * s, 4 * s + 4):
-            k, h = far[n // 2]
-            p = n % 2
-            piece = both[:, (n % 4) * share : (n % 4 + 1) * share]
-            fs_send[n] = piece.astype(BF16)
-            if n < count - 2:
-                fs_copy(n, me, k, 2 * h + p).start()
-            else:
-                total = total + jnp.where(lax.rem(tp, 2) == p, piece, F32(0.0))
-
-                @pl.when(lax.rem(tp, 2) != p)
-                def _():
-                    fs_copy(n, me, k, 2 * h + p).start()
-
-    landed(fs_all.at[pl.ds(0, count - 1)], fs_rs)
-    for d in range(1, count):
-        total = total + fs_all[lax.rem(me + d, count)].astype(F32)
+        b = s % first_own
+        if s < first_own:
+            for q in range(2):
+                fp_send[2 * b + q] = both[:, q * chunk : (q + 1) * chunk].astype(BF16)
+            pair_copy(b, fp_send, fp_all, fp_ss, fp_rs).start()
+        else:
+            landed(fp_all.at[pl.ds(2 * b, 2)], fp_rs.at[b])
+            for q in range(2):
+                k, h = order[chunks // 2 + 2 * b + q]
+                term = both[:, q * chunk : (q + 1) * chunk] + fp_all[2 * b + q].astype(F32)
+                for p in range(2):
+                    n = 4 * b + 2 * q + p
+                    piece = term[:, p * share : (p + 1) * share]
+                    fs_send[n] = piece.astype(BF16)
+                    if n < chunks - 2:
+                        fs_copy(n, k, 2 * h + p).start()
+                    else:
+                        total = total + jnp.where(lax.rem(tp, 2) == p, piece, F32(0.0))
+
+                        @pl.when(lax.rem(tp, 2) != p)
+                        def _():
+                            fs_copy(n, k, 2 * h + p).start()
+
+    landed(fs_all.at[pl.ds(0, sources - 1)], fs_rs)
+    for d in range(1, sources):
+        total = total + fs_all[lax.rem(slot + d, sources)].astype(F32)
     out_ref[...] = total.astype(BF16)
 
     others = pl.ds(0, groups - 1)
     landed(q_all.at[others], q_ss)
     landed(part_all.at[others], part_ss)
     landed(log_all.at[others], log_ss)
-    landed(fs_all.at[pl.ds(0, count - 1)], fs_ss)
+    landed(fs_all.at[pl.ds(0, sources - 1)], fs_ss)
+    landed(rp_all, rp_ss)
+    landed(fp_all, fp_ss)
 
     @pl.when(owns)
     def _():
-        landed(rs_all.at[pl.ds(0, chunks - 1)], rs_ss)
-        landed(rs_all.at[pl.ds(0, count - 1)], ag_ss)
+        landed(rp_all.at[pl.ds(0, chunks // 2 - 1)], rs_ss)
+        rows_sent = (count - 1) * batch * chunk // 128
+        landed(gu_v.at[pl.ds(0, rows_sent), pl.ds(0, 128)], ag_ss)
 
     @pl.when(jnp.logical_not(owns))
     def _():
-        landed(rs_all.at[pl.ds(0, chunks)], rs_ss)
+        landed(rp_all, rs_ss)
 
 
 def per_device(*operands):
@@ -498,6 +535,7 @@
     vmem = pl.BlockSpec(memory_space=pltpu.VMEM)
     anywhere = pl.BlockSpec(memory_space=pl.ANY)
     packed = 2 * (latent + rope)
+    half_set = pltpu.VMEM((chunks // 2, batch, chunk), BF16)
     scratch = [
         pltpu.VMEM((batch, width), BF16),
         pltpu.VMEM((batch, heads, head_dim), BF16),
@@ -523,25 +561,26 @@
         pltpu.VMEM((batch, heads, latent), F32),
         pltpu.VMEM((batch, heads * head_dim), BF16),
         pltpu.VMEM((batch, chunk), F32),
-        pltpu.VMEM((chunks, batch, chunk), BF16),
-        pltpu.VMEM((count, batch, chunk), BF16),
+        half_set, half_set, half_set,
+        pltpu.VMEM((count // 2, batch, chunk), BF16),
         pltpu.VMEM((batch, chunk), BF16),
         pltpu.VMEM((chunks, batch, chunk), BF16),
-        pltpu.VMEM((count, batch, share), BF16),
-        pltpu.VMEM((count, batch, share), BF16),
+        half_set, half_set,
+        pltpu.VMEM((count // 2, batch, share), BF16),
+        pltpu.VMEM((count // 2, batch, share), BF16),
         dma((5,)), dma, dma, dma,
         dma, dma((chunks // 2,)), dma((2,)),
         dma, dma((parts,)), dma, dma((parts,)), dma, dma,
-        dma, dma, dma, dma((chunks,)), dma, dma,
+        dma, dma((chunks // 4,)), dma, dma, dma, dma((chunks,)), dma, dma((chunks // 4,)), dma, dma,
     ]
     return pl.pallas_call(
         functools.partial(layer_kernel, groups, tps, share, chunk, rows, SPAN),
-        out_shape=jax.ShapeDtypeStruct((batch, share), BF16),
+        out_shape=pltpu.VMEM((batch, share), BF16),
         in_specs=[anywhere] * 12,
         out_specs=vmem,
         scratch_shapes=scratch,
         compiler_params=pltpu.CompilerParams(
-            collective_id=0, has_side_effects=True, vmem_limit_bytes=VMEM_BYTES
+            collective_id=0, has_side_effects=True, vmem_limit_bytes=VMEM_BYTES - 640 * 1024
         ),
     )(
         hidden_in, queries_nope, queries_rope, lengths.reshape(1, batch), norm_gain.reshape(1, width),

time: 38.8 us -> 37.7 us (0.972)
  local copies, waits for them, and re-layouts: 1.3 us -> 0.6 us
  Pallas kernels: 37.3 us -> 36.9 us
    unnamed x1, local copies, waits for them, and re-layouts: 1.3 us -> 0.6 us
where the time goes in v3:
time: 37.7 us; the launch traced here: 37.5 us
  Pallas kernels  36.9 us (98%)
  local copies, waits for them, and re-layouts  0.6 us (2%)
    pallas_call x1, Pallas kernels, per_device(): pl.pallas_call(functools.partial(layer_kernel, groups, tps, share, chunk,...  36.9 us

profile of v3, /device:TPU:0, one launch (start us, length us, event | category | flops | bytes accessed | tf_op | source)
XLA Modules:
  0.0 37.5 jit_solution(12000013785534868669)
XLA Ops:
  0.0 36.9 %shard_map.118 = bf16[8,448]{1,0:T(8,128)(2,1)S(1)} custom-call(bf16[8,7168]{1,0:T(8,128)(2,1)} %hidden_hbm.1, bf16[8,8,128]{2,1,0:T(8,128)(2,1)} %nope_hbm.1, bf16[8,8,64]{2,1,0:T(8,128)(2,1)} %rope_hbm.1, s32[1,8]{1,0:T(1,128)} %bitcast.5, f32[1,7168]{1,0:T(1,128)} %bitcast.4, bf16[8,576,384]{2,1,0:T(8,128)(2,1)} %bitcast.3, bf16[8,128,512]{2,1,0:T(8,128)(2,1)} %uk_hbm.1, ...), custom_call_target="tpu_custom_call" | custom-call | tf_op jit(solution)/shard_map/pallas_call | solution.py:576
  36.9 0.6 %copy.14 = bf16[8,448]{1,0:T(8,128)(2,1)} copy(bf16[8,448]{1,0:T(8,128)(2,1)S(1)} %shard_map.118) | data formatting | bytes 14336

commit v4 on v3

--- a/solution.py
+++ b/solution.py
@@ -108,7 +108,7 @@
     nope_s, qlat_s, score_s, weight_s, q_send, q_all, part_send, part_all, log_send, log_all,
     olat_s, head_s, own_s, rp_send, rp_all, rs_send, rs_all, ag_send, ag_all, fp_send, fp_all, fs_send, fs_all,
     in_sem, uk_sem, cache_sem, uv_sem, wo_sem, gu_sem, wd_sem,
-    q_ss, q_rs, part_ss, part_rs, log_ss, log_rs, rp_ss, rp_rs, rs_ss, rs_rs, ag_ss, ag_rs, fp_ss, fp_rs, fs_ss, fs_rs,
+    q_ss, q_rs, part_ss, part_rs, log_ss, log_rs, rp_ss, rp_rs, rs_ss, rs_rs, ag_ss, ag_rs, fp_ss, fp_rs, fs_ss, fs_rs, up_sem, down_sem,
 ):
     count = groups * tps
     kvp = lax.axis_index("kvp")
@@ -200,11 +200,23 @@
     uk_load.start()
     small[1].start()
 
-    @pl.loop(1, count)
-    def _(d):
-        pl.semaphore_signal(
-            barrier, inc=1, device_id=peer(lax.rem(me + d, count)), device_id_type=MESH
-        )
+    below = {"kvp": kvp, "tp": lax.rem(tp + tps - 1, tps)}
+    above = {"kvp": kvp, "tp": lax.rem(tp + 1, tps)}
+    has_below, has_above = tp > 0, tp < tps - 1
+
+    def greet(sem, device):
+        pl.semaphore_signal(sem, inc=1, device_id=device, device_id_type=MESH)
+
+    for i in range(1, groups):
+        greet(barrier, {"kvp": target_of(i), "tp": tp})
+
+    @pl.when(has_below)
+    def _():
+        greet(barrier, below)
+
+    @pl.when(has_above)
+    def _():
+        greet(barrier, above)
 
     cache_load.start()
     for copy in small[2:]:
@@ -228,7 +240,8 @@
     for b in range(batch):
         first = (b % 2) * latent
         q_send[b // 2, :, first : first + latent] = qlat_s[b].astype(BF16)
-    pl.semaphore_wait(barrier, count - 1)
+    edges = (tps - tp - 1) // (tps - 1) + tp // (tps - 1)
+    pl.semaphore_wait(barrier, groups + 1 - edges)
 
     def q_copy(i, u):
         other = target_of(i)
@@ -271,6 +284,28 @@
     steps = chunks // 2
     for s in range(steps // 2):
         load_step(s)
+    def token(sem, arrives, leaves, device):
+        @pl.when(arrives)
+        def _():
+            pl.semaphore_wait(sem, 1)
+
+        @pl.when(leaves)
+        def _():
+            greet(sem, device)
+
+    up = functools.partial(token, up_sem, has_below, has_above, above)
+    down = functools.partial(token, down_sem, has_above, has_below, below)
+
+    @pl.when(half < halves // 2)
+    def _():
+        up()
+        down()
+
+    @pl.when(half >= halves // 2)
+    def _():
+        down()
+        up()
+
     q_all[kvp] = q_send[...]
     for copy in small[2:]:
         copy.wait()
@@ -572,6 +607,7 @@
         dma, dma((chunks // 2,)), dma((2,)),
         dma, dma((parts,)), dma, dma((parts,)), dma, dma,
         dma, dma((chunks // 4,)), dma, dma, dma, dma((chunks,)), dma, dma((chunks // 4,)), dma, dma,
+        pltpu.SemaphoreType.REGULAR, pltpu.SemaphoreType.REGULAR,
     ]
     return pl.pallas_call(
         functools.partial(layer_kernel, groups, tps, share, chunk, rows, SPAN),

time: 37.7 us -> 37.1 us (0.984)
  Pallas kernels: 36.9 us -> 36.3 us
    pallas_call x1, Pallas kernels: 36.9 us -> 36.3 us  [per_device(): pl.pallas_call(functools.partial(layer_kernel, groups, tps, share, chunk,...]
where the time goes in v4:
time: 37.1 us; the launch traced here: 36.9 us
  Pallas kernels  36.3 us (98%)
  local copies, waits for them, and re-layouts  0.6 us (2%)
    pallas_call x1, Pallas kernels, per_device(): pl.pallas_call(functools.partial(layer_kernel, groups, tps, share, chunk,...  36.3 us

profile of v4, /device:TPU:0, one launch (start us, length us, event | category | flops | bytes accessed | tf_op | source)
XLA Modules:
  0.0 36.9 jit_solution(5390745458262892887)
XLA Ops:
  0.0 36.3 %shard_map.118 = bf16[8,448]{1,0:T(8,128)(2,1)S(1)} custom-call(bf16[8,7168]{1,0:T(8,128)(2,1)} %hidden_hbm.1, bf16[8,8,128]{2,1,0:T(8,128)(2,1)} %nope_hbm.1, bf16[8,8,64]{2,1,0:T(8,128)(2,1)} %rope_hbm.1, s32[1,8]{1,0:T(1,128)} %bitcast.5, f32[1,7168]{1,0:T(1,128)} %bitcast.4, bf16[8,576,384]{2,1,0:T(8,128)(2,1)} %bitcast.3, bf16[8,128,512]{2,1,0:T(8,128)(2,1)} %uk_hbm.1, ...), custom_call_target="tpu_custom_call" | custom-call | tf_op jit(solution)/shard_map/pallas_call | solution.py:612
  36.3 0.6 %copy.14 = bf16[8,448]{1,0:T(8,128)(2,1)} copy(bf16[8,448]{1,0:T(8,128)(2,1)S(1)} %shard_map.118) | data formatting | bytes 14336

commit v5 on v4

--- a/solution.py
+++ b/solution.py
@@ -1,4 +1,5 @@
 import functools
+import math
 
 import jax
 import jax.numpy as jnp
@@ -103,12 +104,12 @@
     hidden_hbm, nope_hbm, rope_hbm, len_hbm, gain_hbm,
     cache_hbm, uk_hbm, uv_hbm, wo_hbm, wg_hbm, wu_hbm, wd_hbm,
     out_ref,
-    hidden_v, nope_v, rope_v, len_v, gain_v, gain_s,
+    hidden_v, nope_v, rope_v, len_v, gain_v, gain_s, hid_s,
     cache_v, uk_v, uv_v, big_v, gu_v,
     nope_s, qlat_s, score_s, weight_s, q_send, q_all, part_send, part_all, log_send, log_all,
-    olat_s, head_s, own_s, rp_send, rp_all, rs_send, rs_all, ag_send, ag_all, fp_send, fp_all, fs_send, fs_all,
+    olat_s, head_s, own_s, rs_send, rs_all, ag_send, ag_all, fs_send, fs_all,
     in_sem, uk_sem, cache_sem, uv_sem, wo_sem, gu_sem, wd_sem,
-    q_ss, q_rs, part_ss, part_rs, log_ss, log_rs, rp_ss, rp_rs, rs_ss, rs_rs, ag_ss, ag_rs, fp_ss, fp_rs, fs_ss, fs_rs, up_sem, down_sem,
+    q_ss, q_rs, part_ss, part_rs, log_ss, log_rs, rs_ss, rs_rs, ag_ss, ag_rs, fs_ss, fs_rs, up_sem, down_sem,
 ):
     count = groups * tps
     kvp = lax.axis_index("kvp")
@@ -132,20 +133,18 @@
     def target_of(i):
         return lax.rem(kvp // 2 + i // 2, chips) * 2 + lax.rem(kvp + i, 2)
 
-    def owner_tp(h):
-        return 2 * h + 1 - (4 * h + 2) // tps
-
     near = [
         (target_of(i), lax.rem(half + e, halves)) for e in range(halves) for i in range(groups)
     ]
-    reach = [(e, i) for e in range(halves) for i in range(groups)][::-1]
-    order = [near[e * groups + i] for e, i in reach if i % 2 == 1]
-    order += [near[e * groups + i] for e, i in reach if i % 2 == 0]
-    sibling = {"kvp": target_of(1), "tp": tp}
-    sources = chips * tps
-    slot = (kvp // 2) * tps + tp
-    mine = kvp * halves + half
-    owns = tp == owner_tp(half)
+    far = near[::-1]
+    planes = [tp, tp + 1 - 2 * lax.rem(tp, 2)]
+    for e in range(1, halves):
+        h = lax.rem(half + e, halves)
+        p = (half - h + halves - 1) // halves
+        planes += [2 * h + p, 2 * h + 1 - p]
+    shares = [(target_of(i), z) for z in planes for i in range(groups)]
+    bounds = [0, 2] + list(range(groups, count + 1, groups))
+    segments = list(zip(bounds[:-1], bounds[1:]))
 
     def load(source, target, sem):
         return pltpu.make_async_copy(source, target, sem)
@@ -157,7 +156,7 @@
         return pl.ds((t % 2) * chunk, chunk)
 
     def load_wo(t):
-        k, h = order[t]
+        k, h = far[t]
         return load(
             wo_hbm.at[:, cols(k * halves + h)],
             big_v.at[t // 2, pl.ds(0, out_rows), side(t)],
@@ -165,24 +164,25 @@
         )
 
     def load_wd(t):
-        k, h = order[t]
+        k, h = far[t]
         return load(wd_hbm.at[:, cols(k * halves + h)], big_v.at[t // 2, :, side(t)], wd_sem.at[2 * t // chunks])
 
-    def load_gu(t, n):
-        k, h = near[t]
+    def load_gu(n, t, segment):
+        k, z = shares[t]
+        rows = pl.ds(pl.multiple_of((k * tps + z) * share, math.gcd(share, 128)), share)
         return load(
-            (wg_hbm, wu_hbm)[n].at[cols(k * halves + h)],
-            gu_v.at[pl.ds(t * chunk, chunk), pl.ds(n * hidden_units, hidden_units)],
-            gu_sem.at[t // 2],
+            (wg_hbm, wu_hbm)[n].at[rows],
+            gu_v.at[pl.ds(t * share, share), pl.ds(n * hidden_units, hidden_units)],
+            gu_sem.at[segment],
         )
 
     def landed(ref, sem):
         pltpu.make_async_copy(ref, ref, sem).wait()
 
-    def load_step(s):
-        for t in (2 * s, 2 * s + 1):
-            load_gu(t, 0).start(priority=1)
-            load_gu(t, 1).start(priority=1)
+    def load_segment(segment):
+        for t in range(*segments[segment]):
+            load_gu(0, t, segment).start(priority=1)
+            load_gu(1, t, segment).start(priority=1)
 
     small = [
         load(nope_hbm, nope_v, in_sem.at[0]),
@@ -282,8 +282,9 @@
         for i in outward:
             q_copy(i, u).start()
     steps = chunks // 2
-    for s in range(steps // 2):
-        load_step(s)
+    early = len(segments) // 2 + 1
+    for segment in range(early):
+        load_segment(segment)
     def token(sem, arrives, leaves, device):
         @pl.when(arrives)
         def _():
@@ -309,8 +310,10 @@
     q_all[kvp] = q_send[...]
     for copy in small[2:]:
         copy.wait()
-    for j in range(chunks):
-        gain_s[j] = jnp.broadcast_to(gain_v[:, j * chunk : (j + 1) * chunk], (batch, chunk))
+    for n in range(count):
+        piece = slice(n * share, (n + 1) * share)
+        gain_s[n] = jnp.broadcast_to(gain_v[:, piece], (batch, share))
+        hid_s[n] = hidden_v[:, piece].astype(F32)
     cache_load.wait()
 
     scale = float(head_dim + rope) ** (-0.5)
@@ -352,8 +355,8 @@
         log_send[g] = logs_acc[g * heads : (g + 1) * heads]
     for i in outward:
         log_copy(i).start()
-    for s in range(steps // 2, steps):
-        load_step(s)
+    for segment in range(early, len(segments)):
+        load_segment(segment)
     part_all[kvp] = part_send[kvp]
     log_all[kvp] = log_send[kvp]
     uv_load.wait()
@@ -374,168 +377,107 @@
             olat_s[:, i, :].astype(BF16), uv_v[i], preferred_element_type=F32
         ).astype(BF16)
 
-    def pair_copy(b, source, target, ss, rs):
-        return pltpu.make_async_remote_copy(
-            src_ref=source.at[pl.ds(2 * b, 2)],
-            dst_ref=target.at[pl.ds(2 * b, 2)],
-            send_sem=ss,
-            recv_sem=rs.at[b],
-            device_id=sibling,
-            device_id_type=MESH,
-        )
-
-    def rs_copy(n, k, h):
-        return pltpu.make_async_remote_copy(
-            src_ref=rs_send.at[n],
-            dst_ref=rs_all.at[slot],
-            send_sem=rs_ss,
-            recv_sem=rs_rs,
-            device_id={"kvp": k, "tp": owner_tp(h)},
-            device_id_type=MESH,
-        )
-
-    first_own = steps // 2
-    for s in range(steps):
-        both = jnp.dot(head_s[...], big_v[s, :out_rows], preferred_element_type=F32)
+    def scatter_sum(lhs, depth, total, send, arrived, ss, rs, after):
+        def copy(n, k, z):
+            return pltpu.make_async_remote_copy(
+                src_ref=send.at[n],
+                dst_ref=arrived.at[me],
+                send_sem=ss,
+                recv_sem=rs,
+                device_id={"kvp": k, "tp": z},
+                device_id_type=MESH,
+            )
+
+        for s in range(steps):
+            both = jnp.dot(lhs, big_v[s, :depth], preferred_element_type=F32)
+            after(s)
+            for t in (2 * s, 2 * s + 1):
+                k, h = far[t]
+                pieces = [
+                    both[:, n * share : (n + 1) * share] for n in (2 * (t % 2), 2 * (t % 2) + 1)
+                ]
+                for p in range(2):
+                    send[2 * t + p] = pieces[p].astype(BF16)
+                if t < chunks - 1:
+                    p = (h - half + halves) // halves
+                    copy(2 * t + p, k, 2 * h + p).start()
+                    copy(2 * t + 1 - p, k, 2 * h + 1 - p).start()
+                else:
+                    for p in range(2):
+                        total = total + jnp.where(lax.rem(tp, 2) == p, pieces[p], F32(0.0))
+
+                        @pl.when(lax.rem(tp, 2) != p)
+                        def _():
+                            copy(2 * t + p, k, 2 * h + p).start()
+
+        landed(arrived.at[pl.ds(0, count - 1)], rs)
+        for d in range(1, count):
+            total = total + arrived[lax.rem(me + d, count)].astype(F32)
+        return total
+
+    def reload(s):
         load_wd(2 * s).start(priority=1)
         load_wd(2 * s + 1).start(priority=1)
-        b = s % first_own
-        if s < first_own:
-            for q in range(2):
-                rp_send[2 * b + q] = both[:, q * chunk : (q + 1) * chunk].astype(BF16)
-            pair_copy(b, rp_send, rp_all, rp_ss, rp_rs).start()
-        else:
-            landed(rp_all.at[pl.ds(2 * b, 2)], rp_rs.at[b])
-            for q in range(2):
-                n = 2 * b + q
-                k, h = order[chunks // 2 + n]
-                term = both[:, q * chunk : (q + 1) * chunk] + rp_all[n].astype(F32)
-                rs_send[n] = term.astype(BF16)
-                if n < chunks // 2 - 1:
-                    rs_copy(n, k, h).start()
-                else:
-                    own_s[...] = term
-
-                    @pl.when(jnp.logical_not(owns))
-                    def _():
-                        rs_copy(n, k, h).start()
-
-    def ag_copy(d, j, dest):
-        return pltpu.make_async_remote_copy(
+
+    residual = scatter_sum(
+        head_s[...], out_rows, hid_s[me], rs_send, rs_all, rs_ss, rs_rs, reload
+    )
+    own_s[...] = residual
+    ag_send[...] = residual.astype(BF16)
+    for t in range(1, count):
+        k, z = shares[t]
+        pltpu.make_async_remote_copy(
             src_ref=ag_send,
-            dst_ref=ag_all.at[j],
+            dst_ref=ag_all.at[me],
             send_sem=ag_ss,
-            recv_sem=ag_rs.at[j],
-            device_id=peer(dest),
+            recv_sem=ag_rs.at[0 if t < 2 else 1 if t < groups else 2 + tp],
+            device_id={"kvp": k, "tp": z},
             device_id_type=MESH,
-        )
-
-    @pl.when(owns)
-    def _():
-        residual = hidden_v[:, cols(mine)].astype(F32) + own_s[...]
-        landed(rs_all.at[pl.ds(0, sources - 1)], rs_rs)
-        total = residual
-        for d in range(1, sources):
-            total = total + rs_all[lax.rem(slot + d, sources)].astype(F32)
-        ag_send[...] = total.astype(BF16)
-
-        @pl.loop(1, count)
-        def _(d):
-            ag_copy(d, mine, lax.rem(me + d, count)).start()
-
-        ag_all[mine] = ag_send[...]
+        ).start()
+    ag_all[me] = ag_send[...]
 
     square = jnp.zeros((batch, 1), F32)
-    for s in range(steps):
-        landed(gu_v.at[pl.ds(2 * s * chunk, 2 * chunk)], gu_sem.at[s])
+    for segment in range(len(segments)):
+        landed(
+            gu_v.at[pl.ds(segments[segment][0] * share, (segments[segment][1] - segments[segment][0]) * share)],
+            gu_sem.at[segment],
+        )
     products = jnp.zeros((batch, 2 * hidden_units), F32)
-    for s in range(steps):
+    for segment, (low, high) in enumerate(segments):
+        came = high - low - (segment == 0)
+        landed(
+            ag_all.at[pl.ds(0, came)],
+            ag_rs.at[segment if segment < 2 else 2 + planes[segment - 1]],
+        )
         x = []
-        for t in (2 * s, 2 * s + 1):
-            k, h = near[t]
-            j = k * halves + h
-            if t == 0:
-                @pl.when(jnp.logical_not(owns))
-                def _():
-                    ag_copy(0, j, k * tps + owner_tp(h)).wait_recv()
-            else:
-                ag_copy(0, j, k * tps + owner_tp(h)).wait_recv()
-        for t in (2 * s, 2 * s + 1):
-            k, h = near[t]
-            j = k * halves + h
-            value = ag_all[j].astype(F32)
+        for k, z in shares[low:high]:
+            value = ag_all[k * tps + z].astype(F32)
             square = square + jnp.sum(value * value, axis=1, keepdims=True)
-            x.append((value * gain_s[j]).astype(BF16))
+            x.append((value * gain_s[k * tps + z]).astype(BF16))
         products = products + jnp.dot(
             jnp.concatenate(x, axis=1),
-            gu_v[2 * s * chunk : 2 * (s + 1) * chunk],
+            gu_v[low * share : high * share],
             preferred_element_type=F32,
         )
     products = products * lax.rsqrt(square / width + 1e-06)
     gate, up = products[:, :hidden_units], products[:, hidden_units:]
     act = (gate / (1.0 + jnp.exp(-gate)) * up).astype(BF16)
 
-    def fs_copy(n, k, z):
-        return pltpu.make_async_remote_copy(
-            src_ref=fs_send.at[n],
-            dst_ref=fs_all.at[slot],
-            send_sem=fs_ss,
-            recv_sem=fs_rs,
-            device_id={"kvp": k, "tp": z},
-            device_id_type=MESH,
-        )
-
-    pair = ag_all[mine].astype(F32)
-    total = jnp.where(lax.rem(tp, 2) == 0, pair[:, :share], pair[:, share:])
     for s in range(2):
         landed(big_v.at[pl.ds(s * steps // 2, steps // 2)], wd_sem.at[s])
-    for s in range(steps):
-        both = jnp.dot(act, big_v[s], preferred_element_type=F32)
-        b = s % first_own
-        if s < first_own:
-            for q in range(2):
-                fp_send[2 * b + q] = both[:, q * chunk : (q + 1) * chunk].astype(BF16)
-            pair_copy(b, fp_send, fp_all, fp_ss, fp_rs).start()
-        else:
-            landed(fp_all.at[pl.ds(2 * b, 2)], fp_rs.at[b])
-            for q in range(2):
-                k, h = order[chunks // 2 + 2 * b + q]
-                term = both[:, q * chunk : (q + 1) * chunk] + fp_all[2 * b + q].astype(F32)
-                for p in range(2):
-                    n = 4 * b + 2 * q + p
-                    piece = term[:, p * share : (p + 1) * share]
-                    fs_send[n] = piece.astype(BF16)
-                    if n < chunks - 2:
-                        fs_copy(n, k, 2 * h + p).start()
-                    else:
-                        total = total + jnp.where(lax.rem(tp, 2) == p, piece, F32(0.0))
-
-                        @pl.when(lax.rem(tp, 2) != p)
-                        def _():
-                            fs_copy(n, k, 2 * h + p).start()
-
-    landed(fs_all.at[pl.ds(0, sources - 1)], fs_rs)
-    for d in range(1, sources):
-        total = total + fs_all[lax.rem(slot + d, sources)].astype(F32)
+    total = scatter_sum(
+        act, big_v.shape[1], own_s[...], fs_send, fs_all, fs_ss, fs_rs, lambda s: None
+    )
     out_ref[...] = total.astype(BF16)
 
     others = pl.ds(0, groups - 1)
     landed(q_all.at[others], q_ss)
     landed(part_all.at[others], part_ss)
     landed(log_all.at[others], log_ss)
-    landed(fs_all.at[pl.ds(0, sources - 1)], fs_ss)
-    landed(rp_all, rp_ss)
-    landed(fp_all, fp_ss)
-
-    @pl.when(owns)
-    def _():
-        landed(rp_all.at[pl.ds(0, chunks // 2 - 1)], rs_ss)
-        rows_sent = (count - 1) * batch * chunk // 128
-        landed(gu_v.at[pl.ds(0, rows_sent), pl.ds(0, 128)], ag_ss)
-
-    @pl.when(jnp.logical_not(owns))
-    def _():
-        landed(rp_all, rs_ss)
+    everyone = pl.ds(0, count - 1)
+    landed(rs_all.at[everyone], rs_ss)
+    landed(ag_all.at[everyone], ag_ss)
+    landed(fs_all.at[everyone], fs_ss)
 
 
 def per_device(*operands):
@@ -570,14 +512,15 @@
     vmem = pl.BlockSpec(memory_space=pltpu.VMEM)
     anywhere = pl.BlockSpec(memory_space=pl.ANY)
     packed = 2 * (latent + rope)
-    half_set = pltpu.VMEM((chunks // 2, batch, chunk), BF16)
+    spread = pltpu.VMEM((count, batch, share), BF16)
     scratch = [
         pltpu.VMEM((batch, width), BF16),
         pltpu.VMEM((batch, heads, head_dim), BF16),
         pltpu.VMEM((batch, heads, rope), BF16),
         pltpu.VMEM((1, batch), jnp.int32),
         pltpu.VMEM((1, width + 1024), F32),
-        pltpu.VMEM((chunks, batch, chunk), F32),
+        pltpu.VMEM((count, batch, share), F32),
+        pltpu.VMEM((count, batch, share), F32),
         pltpu.VMEM((batch, latent + rope, ctx), BF16),
         pltpu.VMEM(w_uk.shape, BF16),
         pltpu.VMEM(w_uv.shape, BF16),
@@ -595,18 +538,12 @@
         pltpu.VMEM((groups, heads, 128), F32),
         pltpu.VMEM((batch, heads, latent), F32),
         pltpu.VMEM((batch, heads * head_dim), BF16),
-        pltpu.VMEM((batch, chunk), F32),
-        half_set, half_set, half_set,
-        pltpu.VMEM((count // 2, batch, chunk), BF16),
-        pltpu.VMEM((batch, chunk), BF16),
-        pltpu.VMEM((chunks, batch, chunk), BF16),
-        half_set, half_set,
-        pltpu.VMEM((count // 2, batch, share), BF16),
-        pltpu.VMEM((count // 2, batch, share), BF16),
+        pltpu.VMEM((batch, share), F32),
+        spread, spread, pltpu.VMEM((batch, share), BF16), spread, spread, spread,
         dma((5,)), dma, dma, dma,
-        dma, dma((chunks // 2,)), dma((2,)),
+        dma, dma((tps + 1,)), dma((2,)),
         dma, dma((parts,)), dma, dma((parts,)), dma, dma,
-        dma, dma((chunks // 4,)), dma, dma, dma, dma((chunks,)), dma, dma((chunks // 4,)), dma, dma,
+        dma, dma, dma, dma((tps + 2,)), dma, dma,
         pltpu.SemaphoreType.REGULAR, pltpu.SemaphoreType.REGULAR,
     ]
     return pl.pallas_call(

time: 37.1 us -> 35.4 us (0.954)
  Pallas kernels: 36.3 us -> 34.6 us
    pallas_call x1, Pallas kernels: 36.3 us -> 34.6 us  [per_device(): pl.pallas_call(functools.partial(layer_kernel, groups, tps, share, chunk,...]
where the time goes in v5:
time: 35.4 us; the launch traced here: 35.2 us
  Pallas kernels  34.6 us (98%)
  local copies, waits for them, and re-layouts  0.6 us (2%)
    pallas_call x1, Pallas kernels, per_device(): pl.pallas_call(functools.partial(layer_kernel, groups, tps, share, chunk,...  34.6 us

profile of v5, /device:TPU:0, one launch (start us, length us, event | category | flops | bytes accessed | tf_op | source)
XLA Modules:
  0.0 35.2 jit_solution(12450429138090332259)
XLA Ops:
  0.0 34.6 %shard_map.118 = bf16[8,448]{1,0:T(8,128)(2,1)S(1)} custom-call(bf16[8,7168]{1,0:T(8,128)(2,1)} %hidden_hbm.1, bf16[8,8,128]{2,1,0:T(8,128)(2,1)} %nope_hbm.1, bf16[8,8,64]{2,1,0:T(8,128)(2,1)} %rope_hbm.1, s32[1,8]{1,0:T(1,128)} %bitcast.5, f32[1,7168]{1,0:T(1,128)} %bitcast.4, bf16[8,576,384]{2,1,0:T(8,128)(2,1)} %bitcast.3, bf16[8,128,512]{2,1,0:T(8,128)(2,1)} %uk_hbm.1, ...), custom_call_target="tpu_custom_call" | custom-call | tf_op jit(solution)/shard_map/pallas_call | solution.py:549
  34.6 0.6 %copy.14 = bf16[8,448]{1,0:T(8,128)(2,1)} copy(bf16[8,448]{1,0:T(8,128)(2,1)S(1)} %shard_map.118) | data formatting | bytes 14336

commit v6 on v5

--- a/solution.py
+++ b/solution.py
@@ -143,7 +143,7 @@
         p = (half - h + halves - 1) // halves
         planes += [2 * h + p, 2 * h + 1 - p]
     shares = [(target_of(i), z) for z in planes for i in range(groups)]
-    bounds = [0, 2] + list(range(groups, count + 1, groups))
+    bounds = [0, 2] + list(range(2 * groups, count + 1, 2 * groups))
     segments = list(zip(bounds[:-1], bounds[1:]))
 
     def load(source, target, sem):
@@ -388,27 +388,30 @@
                 device_id_type=MESH,
             )
 
-        for s in range(steps):
-            both = jnp.dot(lhs, big_v[s, :depth], preferred_element_type=F32)
-            after(s)
-            for t in (2 * s, 2 * s + 1):
-                k, h = far[t]
-                pieces = [
-                    both[:, n * share : (n + 1) * share] for n in (2 * (t % 2), 2 * (t % 2) + 1)
-                ]
-                for p in range(2):
-                    send[2 * t + p] = pieces[p].astype(BF16)
-                if t < chunks - 1:
-                    p = (h - half + halves) // halves
-                    copy(2 * t + p, k, 2 * h + p).start()
-                    copy(2 * t + 1 - p, k, 2 * h + 1 - p).start()
-                else:
-                    for p in range(2):
-                        total = total + jnp.where(lax.rem(tp, 2) == p, pieces[p], F32(0.0))
-
-                        @pl.when(lax.rem(tp, 2) != p)
-                        def _():
-                            copy(2 * t + p, k, 2 * h + p).start()
+        run = steps // halves
+        for e in range(halves):
+            blocks = range(e * run, (e + 1) * run)
+            terms = [
+                jnp.dot(lhs, big_v[s, :depth], preferred_element_type=F32) for s in blocks
+            ]
+            for s, term in zip(blocks, terms):
+                for n in range(4):
+                    piece = term[:, n * share : (n + 1) * share]
+                    send[4 * s + n] = piece.astype(BF16)
+                    if 4 * s + n >= count - 2:
+                        total = total + jnp.where(lax.rem(tp, 2) == n % 2, piece, F32(0.0))
+            for s in blocks:
+                for t in (2 * s, 2 * s + 1):
+                    k, h = far[t]
+                    if t < chunks - 1:
+                        p = (h - half + halves) // halves
+                        copy(2 * t + p, k, 2 * h + p).start()
+                        copy(2 * t + 1 - p, k, 2 * h + 1 - p).start()
+                    else:
+                        n = 2 * t + 1 - lax.rem(tp, 2)
+                        copy(n, k, tp + 1 - 2 * lax.rem(tp, 2)).start()
+            for s in blocks:
+                after(s)
 
         landed(arrived.at[pl.ds(0, count - 1)], rs)
         for d in range(1, count):
@@ -437,18 +440,16 @@
     ag_all[me] = ag_send[...]
 
     square = jnp.zeros((batch, 1), F32)
-    for segment in range(len(segments)):
-        landed(
-            gu_v.at[pl.ds(segments[segment][0] * share, (segments[segment][1] - segments[segment][0]) * share)],
-            gu_sem.at[segment],
-        )
     products = jnp.zeros((batch, 2 * hidden_units), F32)
     for segment, (low, high) in enumerate(segments):
-        came = high - low - (segment == 0)
-        landed(
-            ag_all.at[pl.ds(0, came)],
-            ag_rs.at[segment if segment < 2 else 2 + planes[segment - 1]],
-        )
+        landed(gu_v.at[pl.ds(low * share, (high - low) * share)], gu_sem.at[segment])
+        if segment == 0:
+            landed(ag_all.at[pl.ds(0, 1)], ag_rs.at[0])
+        if segment == 1:
+            landed(ag_all.at[pl.ds(0, groups - 2)], ag_rs.at[1])
+        for n in range(tps):
+            if n and low <= n * groups < high:
+                landed(ag_all.at[pl.ds(0, groups)], ag_rs.at[2 + planes[n]])
         x = []
         for k, z in shares[low:high]:
             value = ag_all[k * tps + z].astype(F32)
@@ -541,7 +542,7 @@
         pltpu.VMEM((batch, share), F32),
         spread, spread, pltpu.VMEM((batch, share), BF16), spread, spread, spread,
         dma((5,)), dma, dma, dma,
-        dma, dma((tps + 1,)), dma((2,)),
+        dma, dma((tps // 2 + 1,)), dma((2,)),
         dma, dma((parts,)), dma, dma((parts,)), dma, dma,
         dma, dma, dma, dma((tps + 2,)), dma, dma,
         pltpu.SemaphoreType.REGULAR, pltpu.SemaphoreType.REGULAR,

time: 35.4 us -> 36.7 us (1.037)
  Pallas kernels: 34.6 us -> 35.9 us
    pallas_call x1, Pallas kernels: 34.6 us -> 35.9 us  [per_device(): pl.pallas_call(functools.partial(layer_kernel, groups, tps, share, chunk,...]
where the time goes in v6:
time: 36.7 us; the launch traced here: 36.5 us
  Pallas kernels  35.9 us (98%)
  local copies, waits for them, and re-layouts  0.6 us (2%)
    pallas_call x1, Pallas kernels, per_device(): pl.pallas_call(functools.partial(layer_kernel, groups, tps, share, chunk,...  35.9 us

profile of v6, /device:TPU:0, one launch (start us, length us, event | category | flops | bytes accessed | tf_op | source)
XLA Modules:
  0.0 36.5 jit_solution(4303980862545548883)
XLA Ops:
  0.0 35.9 %shard_map.118 = bf16[8,448]{1,0:T(8,128)(2,1)S(1)} custom-call(bf16[8,7168]{1,0:T(8,128)(2,1)} %hidden_hbm.1, bf16[8,8,128]{2,1,0:T(8,128)(2,1)} %nope_hbm.1, bf16[8,8,64]{2,1,0:T(8,128)(2,1)} %rope_hbm.1, s32[1,8]{1,0:T(1,128)} %bitcast.5, f32[1,7168]{1,0:T(1,128)} %bitcast.4, bf16[8,576,384]{2,1,0:T(8,128)(2,1)} %bitcast.3, bf16[8,128,512]{2,1,0:T(8,128)(2,1)} %uk_hbm.1, ...), custom_call_target="tpu_custom_call" | custom-call | tf_op jit(solution)/shard_map/pallas_call | solution.py:550
  35.9 0.6 %copy.14 = bf16[8,448]{1,0:T(8,128)(2,1)} copy(bf16[8,448]{1,0:T(8,128)(2,1)S(1)} %shard_map.118) | data formatting | bytes 14336

commit v7 on v5

--- a/solution.py
+++ b/solution.py
@@ -153,19 +153,19 @@
         return pl.ds(pl.multiple_of(j * chunk, 128), chunk)
 
     def side(t):
-        return pl.ds((t % 2) * chunk, chunk)
+        return pl.ds((t % groups) * chunk, chunk)
 
     def load_wo(t):
         k, h = far[t]
         return load(
             wo_hbm.at[:, cols(k * halves + h)],
-            big_v.at[t // 2, pl.ds(0, out_rows), side(t)],
+            big_v.at[t // groups, pl.ds(0, out_rows), side(t)],
             wo_sem,
         )
 
     def load_wd(t):
         k, h = far[t]
-        return load(wd_hbm.at[:, cols(k * halves + h)], big_v.at[t // 2, :, side(t)], wd_sem.at[2 * t // chunks])
+        return load(wd_hbm.at[:, cols(k * halves + h)], big_v.at[t // groups, :, side(t)], wd_sem.at[2 * t // chunks])
 
     def load_gu(n, t, segment):
         k, z = shares[t]
@@ -362,16 +362,16 @@
     uv_load.wait()
     landed(big_v.at[:, pl.ds(0, out_rows)], wo_sem)
     landed(log_all.at[pl.ds(0, groups - 1)], log_rs)
+    for u in range(parts):
+        landed(part_all.at[pl.ds(0, groups - 1), pl.ds(u * span, span)], part_rs.at[u])
     logs = [log_all[g] for g in range(groups)]
     highest = functools.reduce(jnp.maximum, logs)
     overall = highest + jnp.log(sum(jnp.exp(x - highest) for x in logs))
     factors = [jnp.exp(x - overall) for x in logs]
-    for u in range(parts):
-        landed(part_all.at[pl.ds(0, groups - 1), pl.ds(u * span, span)], part_rs.at[u])
-        for b in range(u * span, (u + 1) * span):
-            olat_s[b] = sum(
-                factors[g][:, b : b + 1] * part_all[g, b].astype(F32) for g in range(groups)
-            )
+    for b in range(batch):
+        olat_s[b] = sum(
+            factors[g][:, b : b + 1] * part_all[g, b].astype(F32) for g in range(groups)
+        )
     for i in range(heads):
         head_s[:, i * head_dim : (i + 1) * head_dim] = jnp.dot(
             olat_s[:, i, :].astype(BF16), uv_v[i], preferred_element_type=F32
@@ -388,28 +388,40 @@
                 device_id_type=MESH,
             )
 
-        for s in range(steps):
-            both = jnp.dot(lhs, big_v[s, :depth], preferred_element_type=F32)
-            after(s)
-            for t in (2 * s, 2 * s + 1):
+        def leave(source, low, high, origin):
+            for t in range(low // 2, high // 2):
                 k, h = far[t]
-                pieces = [
-                    both[:, n * share : (n + 1) * share] for n in (2 * (t % 2), 2 * (t % 2) + 1)
-                ]
-                for p in range(2):
-                    send[2 * t + p] = pieces[p].astype(BF16)
+                pieces = []
+                for n in (2 * t, 2 * t + 1):
+                    start = (n - origin) * share
+                    pieces.append(source[:, start : start + share])
+                    send[n] = pieces[-1].astype(BF16)
                 if t < chunks - 1:
                     p = (h - half + halves) // halves
                     copy(2 * t + p, k, 2 * h + p).start()
                     copy(2 * t + 1 - p, k, 2 * h + 1 - p).start()
                 else:
                     for p in range(2):
-                        total = total + jnp.where(lax.rem(tp, 2) == p, pieces[p], F32(0.0))
-
                         @pl.when(lax.rem(tp, 2) != p)
                         def _():
                             copy(2 * t + p, k, 2 * h + p).start()
-
+            return pieces
+
+        held = 2 * groups
+        wide = groups * chunk
+        for e in range(halves):
+            cut = wide if e == halves - 1 else (wide // 2 + 511) // 512 * 512
+            done = cut // share // 2 * 2
+            first = jnp.dot(lhs, big_v[e, :depth, :cut], preferred_element_type=F32)
+            last = leave(first, e * held, e * held + done, e * held)
+            if done < held:
+                rest = jnp.dot(lhs, big_v[e, :depth, cut:], preferred_element_type=F32)
+                rest = jnp.concatenate([first[:, done * share :], rest], axis=1)
+                leave(rest, e * held + done, (e + 1) * held, e * held + done)
+        for p in range(2):
+            total = total + jnp.where(lax.rem(tp, 2) == p, last[p], F32(0.0))
+        for s in range(steps):
+            after(s)
         landed(arrived.at[pl.ds(0, count - 1)], rs)
         for d in range(1, count):
             total = total + arrived[lax.rem(me + d, count)].astype(F32)
@@ -437,13 +449,11 @@
     ag_all[me] = ag_send[...]
 
     square = jnp.zeros((batch, 1), F32)
-    for segment in range(len(segments)):
-        landed(
-            gu_v.at[pl.ds(segments[segment][0] * share, (segments[segment][1] - segments[segment][0]) * share)],
-            gu_sem.at[segment],
-        )
-    products = jnp.zeros((batch, 2 * hidden_units), F32)
+    even = 2 * hidden_units // 512 * 512
+    main = jnp.zeros((batch, even), F32)
+    tail = jnp.zeros((batch, 2 * hidden_units - even), F32)
     for segment, (low, high) in enumerate(segments):
+        landed(gu_v.at[pl.ds(low * share, (high - low) * share)], gu_sem.at[segment])
         came = high - low - (segment == 0)
         landed(
             ag_all.at[pl.ds(0, came)],
@@ -454,17 +464,25 @@
             value = ag_all[k * tps + z].astype(F32)
             square = square + jnp.sum(value * value, axis=1, keepdims=True)
             x.append((value * gain_s[k * tps + z]).astype(BF16))
-        products = products + jnp.dot(
+        main = main + jnp.dot(
             jnp.concatenate(x, axis=1),
-            gu_v[low * share : high * share],
+            gu_v[low * share : high * share, :even],
             preferred_element_type=F32,
         )
+        middle = (low + high) // 2
+        for part, a, b in ((x[: middle - low], low, middle), (x[middle - low :], middle, high)):
+            tail = tail + jnp.dot(
+                jnp.concatenate(part, axis=1),
+                gu_v[a * share : b * share, even:],
+                preferred_element_type=F32,
+            )
+    products = jnp.concatenate([main, tail], axis=1)
     products = products * lax.rsqrt(square / width + 1e-06)
     gate, up = products[:, :hidden_units], products[:, hidden_units:]
     act = (gate / (1.0 + jnp.exp(-gate)) * up).astype(BF16)
 
     for s in range(2):
-        landed(big_v.at[pl.ds(s * steps // 2, steps // 2)], wd_sem.at[s])
+        landed(big_v.at[pl.ds(s * halves // 2, halves // 2)], wd_sem.at[s])
     total = scatter_sum(
         act, big_v.shape[1], own_s[...], fs_send, fs_all, fs_ss, fs_rs, lambda s: None
     )
@@ -524,7 +542,7 @@
         pltpu.VMEM((batch, latent + rope, ctx), BF16),
         pltpu.VMEM(w_uk.shape, BF16),
         pltpu.VMEM(w_uv.shape, BF16),
-        pltpu.VMEM((chunks // 2, ff, 2 * chunk), BF16),
+        pltpu.VMEM((tps // 2, ff, groups * chunk), BF16),
         pltpu.VMEM((width, 2 * ff), BF16),
         pltpu.VMEM((batch, heads, head_dim), F32),
         pltpu.VMEM((batch, heads, latent), F32),

time: 35.4 us -> 35.1 us (level)
  no operation moved by 1% of the time
where the time goes in v7:
time: 35.1 us; the launch traced here: 34.9 us
  Pallas kernels  34.3 us (98%)
  local copies, waits for them, and re-layouts  0.6 us (2%)
    pallas_call x1, Pallas kernels, per_device(): pl.pallas_call(functools.partial(layer_kernel, groups, tps, share, chunk,...  34.3 us

profile of v7, /device:TPU:0, one launch (start us, length us, event | category | flops | bytes accessed | tf_op | source)
XLA Modules:
  0.0 34.9 jit_solution(5299940072142991466)
XLA Ops:
  0.0 34.3 %shard_map.118 = bf16[8,448]{1,0:T(8,128)(2,1)S(1)} custom-call(bf16[8,7168]{1,0:T(8,128)(2,1)} %hidden_hbm.1, bf16[8,8,128]{2,1,0:T(8,128)(2,1)} %nope_hbm.1, bf16[8,8,64]{2,1,0:T(8,128)(2,1)} %rope_hbm.1, s32[1,8]{1,0:T(1,128)} %bitcast.5, f32[1,7168]{1,0:T(1,128)} %bitcast.4, bf16[8,576,384]{2,1,0:T(8,128)(2,1)} %bitcast.3, bf16[8,128,512]{2,1,0:T(8,128)(2,1)} %uk_hbm.1, ...), custom_call_target="tpu_custom_call" | custom-call | tf_op jit(solution)/shard_map/pallas_call | solution.py:567
  34.3 0.6 %copy.14 = bf16[8,448]{1,0:T(8,128)(2,1)} copy(bf16[8,448]{1,0:T(8,128)(2,1)S(1)} %shard_map.118) | data formatting | bytes 14336

commit v8 on v7

--- a/solution.py
+++ b/solution.py
@@ -449,9 +449,8 @@
     ag_all[me] = ag_send[...]
 
     square = jnp.zeros((batch, 1), F32)
-    even = 2 * hidden_units // 512 * 512
-    main = jnp.zeros((batch, even), F32)
-    tail = jnp.zeros((batch, 2 * hidden_units - even), F32)
+    gate = jnp.zeros((batch, hidden_units), F32)
+    up = jnp.zeros((batch, hidden_units), F32)
     for segment, (low, high) in enumerate(segments):
         landed(gu_v.at[pl.ds(low * share, (high - low) * share)], gu_sem.at[segment])
         came = high - low - (segment == 0)
@@ -464,19 +463,11 @@
             value = ag_all[k * tps + z].astype(F32)
             square = square + jnp.sum(value * value, axis=1, keepdims=True)
             x.append((value * gain_s[k * tps + z]).astype(BF16))
-        main = main + jnp.dot(
-            jnp.concatenate(x, axis=1),
-            gu_v[low * share : high * share, :even],
-            preferred_element_type=F32,
-        )
-        middle = (low + high) // 2
-        for part, a, b in ((x[: middle - low], low, middle), (x[middle - low :], middle, high)):
-            tail = tail + jnp.dot(
-                jnp.concatenate(part, axis=1),
-                gu_v[a * share : b * share, even:],
-                preferred_element_type=F32,
-            )
-    products = jnp.concatenate([main, tail], axis=1)
+        x = jnp.concatenate(x, axis=1)
+        rows_used = slice(low * share, high * share)
+        gate = gate + jnp.dot(x, gu_v[rows_used, :hidden_units], preferred_element_type=F32)
+        up = up + jnp.dot(x, gu_v[rows_used, hidden_units:], preferred_element_type=F32)
+    products = jnp.concatenate([gate, up], axis=1)
     products = products * lax.rsqrt(square / width + 1e-06)
     gate, up = products[:, :hidden_units], products[:, hidden_units:]
     act = (gate / (1.0 + jnp.exp(-gate)) * up).astype(BF16)

time: 35.1 us -> 34.5 us (0.983)
  Pallas kernels: 34.3 us -> 33.6 us
    pallas_call x1, Pallas kernels: 34.3 us -> 33.6 us  [per_device(): pl.pallas_call(functools.partial(layer_kernel, groups, tps, share, chunk,...]
where the time goes in v8:
time: 34.5 us; the launch traced here: 34.2 us
  Pallas kernels  33.6 us (97%)
  local copies, waits for them, and re-layouts  0.6 us (2%)
    pallas_call x1, Pallas kernels, per_device(): pl.pallas_call(functools.partial(layer_kernel, groups, tps, share, chunk,...  33.6 us

profile of v8, /device:TPU:0, one launch (start us, length us, event | category | flops | bytes accessed | tf_op | source)
XLA Modules:
  0.0 34.2 jit_solution(14882711455404865597)
XLA Ops:
  0.0 33.6 %shard_map.118 = bf16[8,448]{1,0:T(8,128)(2,1)S(1)} custom-call(bf16[8,7168]{1,0:T(8,128)(2,1)} %hidden_hbm.1, bf16[8,8,128]{2,1,0:T(8,128)(2,1)} %nope_hbm.1, bf16[8,8,64]{2,1,0:T(8,128)(2,1)} %rope_hbm.1, s32[1,8]{1,0:T(1,128)} %bitcast.5, f32[1,7168]{1,0:T(1,128)} %bitcast.4, bf16[8,576,384]{2,1,0:T(8,128)(2,1)} %bitcast.3, bf16[8,128,512]{2,1,0:T(8,128)(2,1)} %uk_hbm.1, ...), custom_call_target="tpu_custom_call" | custom-call | tf_op jit(solution)/shard_map/pallas_call | solution.py:558
  33.6 0.6 %copy.14 = bf16[8,448]{1,0:T(8,128)(2,1)} copy(bf16[8,448]{1,0:T(8,128)(2,1)S(1)} %shard_map.118) | data formatting | bytes 14336
